TPU v7x, 16 devices: a whole 2x2x2 slice. The times are simulated.
16 devices in a mesh: dp: 2 (over z), fsdp: 8 (over y, x, core).
Axes of the slice: x: 2, y: 2, z: 2, core: 2. Of those that a mesh axis runs over, the one named last changes fastest.
Arguments:
- tok_ids: int32 [48, 512], P(('dp', 'fsdp')), parts along dimension 0
- grad_out: bfloat16 [48, 512, 2048], P(('dp', 'fsdp')), parts along dimension 0
- emb_table: bfloat16 [102400, 2048], P('fsdp')
- norm_gain: bfloat16 [2048], P('fsdp')
- w_query: bfloat16 [2048, 3072], P('fsdp')
- w_kv_down: bfloat16 [2048, 576], P('fsdp')
- kv_gain: bfloat16 [512], P('fsdp')
- w_kv_up: bfloat16 [512, 4096], P('fsdp')
- w_out: bfloat16 [2048, 2048], P('fsdp')
Outputs:
- output 1: bfloat16 [48, 512, 2048], P(('dp', 'fsdp')), parts along dimension 0
- output 2: bfloat16 [204800, 2048], P(('dp', 'fsdp')), parts along dimension 0
- output 3: float32 [4096], P(('dp', 'fsdp')), parts along dimension 0
- output 4: float32 [4096, 3072], P(('dp', 'fsdp')), parts along dimension 0
- output 5: float32 [4096, 576], P(('dp', 'fsdp')), parts along dimension 0
- output 6: float32 [1024], P(('dp', 'fsdp')), parts along dimension 0
- output 7: float32 [1024, 4096], P(('dp', 'fsdp')), parts along dimension 0
- output 8: float32 [4096, 2048], P(('dp', 'fsdp')), parts along dimension 0
There are 2 independent parts. A program takes and returns all parts, laid end to end along the dimension named above; an argument that names none is the same for every part.
All inputs are finite; a program needn't handle non-finite values.
Results may differ from a plain program's by a relative error of at most 0.0124488.
Values are sent between devices in bfloat16 or wider.
A program may use at most 1 GiB of HBM per device.

v0:
```python
import math
import jax
import jax.numpy as jnp
from jax import lax
from jax.sharding import PartitionSpec as P

NOPE_DIM = 128
ROPE_DIM = 64
VALUE_DIM = 128
ROPE_THETA = 50000.0
RMS_EPS = 1e-6
ATTN_SCALE = (NOPE_DIM + ROPE_DIM) ** -0.5 * (0.1 * math.log(32.0) + 1.0) ** 2
ROW_DIMS = (((0,), (0,)), ((), ()))
COL_DIMS = (((1,), (1,)), ((), ()))


def rms_scale(in_vals, gain_vec):
    vals_f32 = in_vals.astype(jnp.float32)
    inv_rms = lax.rsqrt(jnp.mean(vals_f32 * vals_f32, axis=-1, keepdims=True) + RMS_EPS)
    return (vals_f32 * inv_rms * gain_vec).astype(jnp.bfloat16)


def rope_tables(seq_len):
    positions = jnp.arange(seq_len, dtype=jnp.float32)
    inv_freq = ROPE_THETA ** (-2.0 * jnp.arange(ROPE_DIM // 2, dtype=jnp.float32) / ROPE_DIM)
    rot_angle = positions[:, None] * inv_freq[None, :]
    rot_angle = jnp.concatenate([rot_angle, rot_angle], axis=-1)
    return jnp.cos(rot_angle), jnp.sin(rot_angle)


def apply_rope(in_vals, cos_tab, sin_tab):
    half_dim = ROPE_DIM // 2
    vals_f32 = in_vals.astype(jnp.float32)
    turned = jnp.concatenate([-vals_f32[..., half_dim:], vals_f32[..., :half_dim]], axis=-1)
    return (vals_f32 * cos_tab + turned * sin_tab).astype(jnp.bfloat16)


def attend_local(q_proj, pe_raw, kv_up):
    seq_len = q_proj.shape[1]
    cos_tab, sin_tab = rope_tables(seq_len)
    q_rot = apply_rope(q_proj[..., NOPE_DIM:], cos_tab[:, None, :], sin_tab[:, None, :])
    k_rot = apply_rope(pe_raw, cos_tab, sin_tab)
    scores = jnp.einsum('bshd,bthd->bhst', q_proj[..., :NOPE_DIM], kv_up[..., :NOPE_DIM], preferred_element_type=jnp.float32)
    scores = scores + jnp.einsum('bshd,btd->bhst', q_rot, k_rot, preferred_element_type=jnp.float32)
    positions = jnp.arange(seq_len)
    causal = positions[:, None] >= positions[None, :]
    scores = jnp.where(causal, scores * ATTN_SCALE, -1e30)
    attn_probs = jax.nn.softmax(scores, axis=-1).astype(jnp.bfloat16)
    attn_mix = jnp.einsum('bhst,bthd->bshd', attn_probs, kv_up[..., NOPE_DIM:], preferred_element_type=jnp.float32)
    return attn_mix.astype(jnp.bfloat16)


def block_step(tok_rows, grad_rows, full_weights, seq_count):
    gain_vec, w_query, w_kv_down, kv_gain, w_kv_up, w_out = full_weights
    kv_rank = kv_gain.shape[0]
    tok_count = tok_rows.shape[0]
    seq_len = tok_count // seq_count
    rows_f32 = tok_rows.astype(jnp.float32)
    normed, norm_pull = jax.vjp(rms_scale, rows_f32, gain_vec.astype(jnp.float32))
    q_proj = jnp.dot(normed, w_query, preferred_element_type=jnp.float32).astype(jnp.bfloat16)
    kv_down = jnp.dot(normed, w_kv_down, preferred_element_type=jnp.float32).astype(jnp.bfloat16)
    latent, latent_pull = jax.vjp(rms_scale, kv_down[:, :kv_rank], kv_gain.astype(jnp.float32))
    kv_up = jnp.dot(latent, w_kv_up, preferred_element_type=jnp.float32).astype(jnp.bfloat16)
    attn_mix, attn_pull = jax.vjp(attend_local, q_proj.reshape(seq_count, seq_len, -1, NOPE_DIM + ROPE_DIM), kv_down[:, kv_rank:].reshape(seq_count, seq_len, ROPE_DIM), kv_up.reshape(seq_count, seq_len, -1, NOPE_DIM + VALUE_DIM))
    mix_rows = attn_mix.reshape(tok_count, -1)
    out_f32 = rows_f32 + jnp.dot(mix_rows, w_out, preferred_element_type=jnp.float32)
    d_w_out = lax.dot_general(mix_rows, grad_rows, ROW_DIMS, preferred_element_type=jnp.float32)
    d_mix = lax.dot_general(grad_rows, w_out, COL_DIMS, preferred_element_type=jnp.float32).astype(jnp.bfloat16)
    d_query, d_pe, d_up = attn_pull(d_mix.reshape(attn_mix.shape))
    d_query = d_query.reshape(tok_count, -1)
    d_up = d_up.reshape(tok_count, -1)
    d_w_kv_up = lax.dot_general(latent, d_up, ROW_DIMS, preferred_element_type=jnp.float32)
    d_latent = lax.dot_general(d_up, w_kv_up, COL_DIMS, preferred_element_type=jnp.float32).astype(jnp.bfloat16)
    d_ckv, d_kv_gain = latent_pull(d_latent)
    d_down = jnp.concatenate([d_ckv, d_pe.reshape(tok_count, ROPE_DIM)], axis=1)
    d_w_kv_down = lax.dot_general(normed, d_down, ROW_DIMS, preferred_element_type=jnp.float32)
    d_w_query = lax.dot_general(normed, d_query, ROW_DIMS, preferred_element_type=jnp.float32)
    d_normed = lax.dot_general(d_query, w_query, COL_DIMS, preferred_element_type=jnp.float32)
    d_normed = d_normed + lax.dot_general(d_down, w_kv_down, COL_DIMS, preferred_element_type=jnp.float32)
    d_rows, d_gain = norm_pull(d_normed.astype(jnp.bfloat16))
    d_rows = d_rows + grad_rows.astype(jnp.float32)
    return out_f32.astype(jnp.bfloat16), d_rows, (d_gain, d_w_query, d_w_kv_down, d_kv_gain, d_w_kv_up, d_w_out)


def solution(mesh):
    tok_spec = P(('dp', 'fsdp'), None)
    seq_spec = P(('dp', 'fsdp'), None, None)
    part_vec = P(('dp', 'fsdp'))
    vec_spec = P('fsdp')
    mat_spec = P('fsdp', None)

    def device_step(tok_ids, grad_out, emb_table, norm_gain, w_query, w_kv_down, kv_gain, w_kv_up, w_out):
        seq_count, seq_len = tok_ids.shape
        vocab_dev, d_model = emb_table.shape
        tok_count = seq_count * seq_len
        all_ids = lax.all_gather(tok_ids.reshape(tok_count), 'fsdp', tiled=True)
        local_ids = all_ids - lax.axis_index('fsdp') * vocab_dev
        is_owned = (local_ids >= 0) & (local_ids < vocab_dev)
        picked = jnp.take(emb_table, jnp.where(is_owned, local_ids, 0), axis=0)
        picked = jnp.where(is_owned[:, None], picked, jnp.zeros((), picked.dtype))
        tok_rows = lax.psum_scatter(picked, 'fsdp', scatter_dimension=0, tiled=True)
        full_weights = tuple(lax.all_gather(shard_piece, 'fsdp', tiled=True) for shard_piece in (norm_gain, w_query, w_kv_down, kv_gain, w_kv_up, w_out))
        block_out, d_rows, weight_grads = block_step(tok_rows, grad_out.reshape(tok_count, d_model), full_weights, seq_count)
        all_grads = lax.all_gather(d_rows, 'fsdp', tiled=True)
        seg_ids = jnp.where(is_owned, local_ids, vocab_dev)
        grad_table = jax.ops.segment_sum(all_grads, seg_ids, num_segments=vocab_dev).astype(jnp.bfloat16)
        grad_shards = tuple(lax.psum_scatter(full_grad, 'fsdp', scatter_dimension=0, tiled=True) for full_grad in weight_grads)
        return (block_out.reshape(seq_count, seq_len, d_model), grad_table) + grad_shards

    return jax.shard_map(device_step, mesh=mesh, in_specs=(tok_spec, seq_spec, mat_spec, vec_spec, mat_spec, mat_spec, vec_spec, mat_spec, mat_spec), out_specs=(seq_spec, tok_spec, part_vec, tok_spec, tok_spec, part_vec, tok_spec, tok_spec), check_vma=False)
```

profile of v0, /device:TPU:0, one launch (start us, length us, event | category | flops | bytes accessed | tf_op | source)
XLA Modules:
  0.0 2479.3 jit_solution(17648162608254239409)
XLA Ops:
  20.2 444.4 %gather_fusion = bf16[12288,2048]{1,0:T(8,128)(2,1)} fusion(bf16[12800,2048]{1,0:T(8,128)(2,1)} %param.11, s32[12288]{0:T(1024)S(1)} %get-tuple-element.33), kind=kCustom, calls=%fused_computation | custom fusion | bytes 100712448 | tf_op jit(solution)/shard_map/jit(_take)/gather | solution.py:99
  464.6 33.8 %select_select_fusion = bf16[12288,2048]{1,0:T(8,128)(2,1)} fusion(bf16[12288,2048]{1,0:T(8,128)(2,1)} %gather_fusion, pred[12288]{0:T(1024)(128)(4,1)S(1)} %get-tuple-element.35, pred[12288]{0:T(1024)(128)(4,1)S(1)} %get-tuple-element.34), kind=kLoop, calls=%fused_computation.30 | loop fusion | flops 50331648 | bytes 100687872 | tf_op jit(solution)/shard_map/jit(_where)/select_n | solution.py:100
  503.6 209.4 %all-reduce.8 = bf16[512]{0:T(512)(128)(2,1)S(1)} all-reduce(bf16[512]{0:T(512)(128)(2,1)S(1)} %dynamic-update-slice), channel_id=1, replica_groups=mesh['dp'=2,'fsdp'=8] {'fsdp'}, use_global_device_ids=true, to_apply=%add.8 | all-reduce | flops 512 | bytes 2048
  721.8 19.7 fusion.65
  757.1 216.6 %reduce-scatter.6.cloned.1.call-done = bf16[1536,2048]{1,0:T(8,128)(2,1)} async-done(((bf16[12288,2048]{1,0:T(8,128)(2,1)}), bf16[1536,2048]{1,0:T(8,128)(2,1)}) %reduce-scatter.6.cloned.1.call-update) | async-done | bytes 6291472 | tf_op jit(solution)/shard_map/reduce_scatter | solution.py:101
  978.4 65.4 %all-gather.12.cloned.1.call-done = bf16[2048,3072]{1,0:T(8,128)(2,1)} async-done(((bf16[256,3072]{1,0:T(8,128)(2,1)}), bf16[2048,3072]{1,0:T(8,128)(2,1)}) %all-gather.12.cloned.1.call-update) | async-done | bytes 12582928 | tf_op jit(solution)/shard_map/all_gather | solution.py:102
  1043.9 26.4 %convolution_convert_fusion.2 = bf16[1536,3072]{1,0:T(8,128)(2,1)} fusion(bf16[2048,3072]{1,0:T(8,128)(2,1)} %all-gather.12.cloned.1.call-done, bf16[1536,2048]{1,0:T(8,128)(2,1)} %reduce-scatter.6.cloned.1.call-done, f32[2048]{0:T(1024)S(1)} %bitcast.148, f32[1536]{0:T(1024)S(1)} %fusion.80), kind=kOutput, calls=%fused_computation.52 | convolution fusion | flops 19344654336 | bytes 28325888 | tf_op jit(solution)/shard_map/dot_general | solution.py:60
  1070.3 21.5 reshape.193
  1163.1 22.2 fusion.98
  1185.3 54.7 %fusion.91 = (f32[3,16,512]{2,1,0:T(8,128)S(1)}, f32[3,16,512,512]{2,3,1,0:T(8,128)}, f32[3,16,512,512]{2,3,1,0:T(8,128)}) fusion(f32[3,512,512,16]{2,1,3,0:T(8,128)} %fusion.98, pred[512,512]{0,1:T(8,128)(4,1)S(1)} %copy-done.4, bf16[3,512,16,128]{3,2,1,0:T(8,128)(2,1)} %get-tuple-element.20, bf16[3,512,16,128]{3,2,1,0:T(8,128)(2,1)} %slice.46), kind=kOutput, calls=%fused_computation.145 | convolution fusion | flops 3271532544 | bytes 163938304 | tf_op jit(solution)/shard_map/jvp(bshd,bthd->bhst)/dot_general | solution.py:43
  1240.0 19.2 fusion.23
  1259.3 38.8 %fusion.11 = (f32[3,16,512]{2,1,0:T(8,128)S(1)}, bf16[3,16,512,512]{2,3,1,0:T(8,128)(2,1)}, bf16[3,16,512,512]{2,3,1,0:T(8,128)(2,1)}) fusion(f32[3,16,512,512]{2,3,1,0:T(8,128)} %get-tuple-element.17, f32[3,16,512]{2,1,0:T(8,128)S(1)} %multiply_divide_fusion, f32[3,16,512]{2,1,0:T(8,128)S(1)} %get-tuple-element.16, f32[3,16,512]{2,1,0:T(8,128)S(1)} %fusion.23, ...), kind=kOutput, calls=%fused_computation.14 | convolution fusion | flops 3321864192 | bytes 113639424 | tf_op jit(solution)/shard_map/transpose(jvp(bhst,bthd->bshd))/dot_general | solution.py:49
  1298.8 49.9 %fusion.16 = bf16[3,512,512,16]{2,1,3,0:T(8,128)(2,1)} fusion(bf16[3,16,512,512]{2,3,1,0:T(8,128)(2,1)} %get-tuple-element.39, f32[3,512,512,16]{2,1,3,0:T(8,128)} %fusion.98, f32[3,16,512,512]{2,3,1,0:T(8,128)} %get-tuple-element.38, f32[3,512,16]{1,2,0:T(8,128)} %bitcast.141, f32[3,512,16]{1,2,0:T(8,128)S(1)} %get-tuple-element.29, ...), kind=kLoop, calls=%fused_computation.19 | loop fusion | flops 138412032 | bytes 151552000 | tf_op jit(solution)/shard_map/transpose(jvp())/mul | solution.py:47
  1375.5 31.9 %convert_bitcast_fusion.1 = bf16[3,512,16,128]{1,3,2,0:T(8,128)(2,1)} fusion(bf16[3,512,16,128]{3,2,1,0:T(8,128)(2,1)} %slice.46, bf16[3,16,512,512]{2,3,1,0:T(8,128)(2,1)} %get-tuple-element.39, f32[3,16,512,512]{2,3,1,0:T(8,128)} %get-tuple-element.17, f32[3,16,512]{2,1,0:T(8,128)S(1)} %copy-done.25, f32[3,16,512]{2,1,0:T(8,128)S(1)} %copy-done.23, ...), kind=kOutput, calls=%fused_computation.69 | convolution fusion | flops 3312451584 | bytes 88637440 | tf_op jit(solution)/shard_map/transpose(jvp(bshd,bthd->bhst))/dot_general | solution.py:43
  1407.4 33.3 %convert_bitcast_fusion.3 = bf16[3,512,16,128]{1,3,2,0:T(8,128)(2,1)} fusion(bf16[3,512,16,128]{3,2,1,0:T(8,128)(2,1)} %get-tuple-element.20, bf16[3,16,512,512]{2,3,1,0:T(8,128)(2,1)} %get-tuple-element.39, f32[3,16,512,512]{2,3,1,0:T(8,128)} %get-tuple-element.17, f32[3,16,512]{2,1,0:T(8,128)S(1)} %copy-done.25, f32[3,16,512]{2,1,0:T(8,128)S(1)} %copy-done.23, ...), kind=kOutput, calls=%fused_computation.71 | convolution fusion | flops 3312451584 | bytes 88637440 | tf_op jit(solution)/shard_map/transpose(jvp(bshd,bthd->bhst))/dot_general | solution.py:43
  1531.3 20.2 reshape.198
  1564.3 31.2 %fusion.27 = (f32[2048]{0:T(1024)S(1)}, f32[1536]{0:T(1024)S(1)}, bf16[1536,2048]{1,0:T(8,128)(2,1)}) fusion(bf16[1536,2048]{1,0:T(8,128)(2,1)S(1)} %bitcast.128, f32[1536]{0:T(1024)S(1)} %copy-done.35, f32[2048]{0:T(1024)S(1)} %bitcast.150, f32[1536,2048]{1,0:T(8,128)} %fusion.69, bf16[1536,3072]{1,0:T(8,128)(2,1)} %reshape.198, ...), kind=kOutput, calls=%fused_computation.45 | convolution fusion | flops 19358806016 | bytes 47214592 | tf_op jit(solution)/shard_map/dot_general | solution.py:78
  1659.3 20.5 fusion.35
  1679.9 28.8 %fusion.85 = f32[2048,3072]{1,0:T(8,128)} fusion(bf16[1536,3072]{1,0:T(8,128)(2,1)} %reshape.198, bf16[1536,2048]{1,0:T(8,128)(2,1)} %reduce-scatter.6.cloned.1.call-done, f32[2048]{0:T(1024)S(1)} %bitcast.153, f32[1536]{0:T(1024)S(1)} %copy-done.35), kind=kOutput, calls=%fused_computation.144 | convolution fusion | flops 19339935744 | bytes 40908800 | tf_op jit(solution)/shard_map/dot_general | solution.py:77
  1718.3 26.6 %all-reduce.11 = (f32[2048]{0:T(1024)S(1)}, f32[512]{0:T(512)S(1)}) all-reduce(f32[2048]{0:T(1024)S(1)} %get-tuple-element.10, f32[512]{0:T(512)S(1)} %copy-done.38), channel_id=3, replica_groups=mesh['dp'=2,'fsdp'=8] {'fsdp'}, use_global_device_ids=true, to_apply=%region_10.11.clone | all-reduce | flops 2560 | bytes 20480
  1746.1 20.3 fusion.30
  1766.4 282.8 %all-gather.16.cloned.1.call-done = f32[12288,2048]{1,0:T(8,128)} async-done(((f32[1536,2048]{1,0:T(8,128)}), f32[12288,2048]{1,0:T(8,128)}) %all-gather.16.cloned.1.call-update) | async-done | bytes 100663312 | tf_op jit(solution)/shard_map/all_gather | solution.py:104
  2049.1 371.7 %scatter_custom_fusion = f32[12800,2048]{1,0:T(8,128)} fusion(s32[12288]{0:T(1024)S(1)} %get-tuple-element.8, f32[12288,2048]{1,0:T(8,128)} %all-gather.16.cloned.1.call-done, s32[12288]{0:T(1024)S(1)} %broadcast_clamp_fusion, f32[]{:T(128)} %constant.23.clone.1), kind=kCustom, calls=%fused_computation.3 | custom fusion | flops 25165824 | bytes 104858112 | tf_op jit(solution)/shard_map/scatter-add | solution.py:106
  2420.9 51.3 %convert_element_type.170 = bf16[12800,2048]{1,0:T(8,128)(2,1)} convert(f32[12800,2048]{1,0:T(8,128)} %scatter_custom_fusion) | non-fusion elementwise | flops 26214400 | bytes 157286400 | tf_op jit(solution)/shard_map/convert_element_type | solution.py:106
  (192 shorter events, 321.6 us)
Async XLA Ops:
  7.2 714.7 %all-gather.14.cloned.1.call-start = ((), (), s32[]{:S(2)}) async-start(), calls=%async_computation.9 | async-start | bytes 9437184 | tf_op jit(solution)/shard_map/all_gather | solution.py:102
  7.9 965.8 %reduce-scatter.6.cloned.1.call-start = ((), (), s32[]{:S(2)}) async-start(), calls=%async_computation.5 | async-start | bytes 56623104 | tf_op jit(solution)/shard_map/reduce_scatter | solution.py:101
  498.5 545.4 %all-gather.12.cloned.1.call-start = ((), (), s32[]{:S(2)}) async-start(), calls=%async_computation.8 | async-start | bytes 14155776 | tf_op jit(solution)/shard_map/all_gather | solution.py:102
  499.2 617.3 %all-gather.8.cloned.1.call-start = ((), (), s32[]{:S(2)}) async-start(), calls=%async_computation.6 | async-start | bytes 2654208 | tf_op jit(solution)/shard_map/all_gather | solution.py:102
  499.8 629.2 %all-gather.10.cloned.1.call-start = ((), (), s32[]{:S(2)}) async-start(), calls=%async_computation.7 | async-start | bytes 4718592 | tf_op jit(solution)/shard_map/all_gather | solution.py:102
  500.4 1548.7 %all-gather.16.cloned.1.call-start = ((), (), s32[]{:S(2)}) async-start(), calls=%async_computation.10 | async-start | bytes 113246208 | tf_op jit(solution)/shard_map/all_gather | solution.py:104
  713.0 416.1 %copy-start.36 = (f32[512]{0:T(512)}, f32[512]{0:T(512)S(1)}, u32[]{:S(2)}) copy-start(f32[512]{0:T(512)S(1)} %convert_element_type.134) | copy-start | bytes 6148
  721.4 395.1 %copy-start.32 = (f32[8,1,256]{2,1,0:T(1,128)}, f32[8,1,256]{2,1,0:T(1,128)S(1)}, u32[]{:S(2)}) copy-start(f32[8,1,256]{2,1,0:T(1,128)S(1)} %convert_element_type.173) | copy-start | bytes 24580
  721.8 436.6 %copy-start.8 = (f32[512,64]{0,1:T(8,128)}, f32[512,64]{0,1:T(8,128)S(1)}, u32[]{:S(2)}) copy-start(f32[512,64]{0,1:T(8,128)S(1)} %get-tuple-element.31) | copy-start | bytes 393220
  721.8 436.5 %copy-start.13 = (f32[512,64]{0,1:T(8,128)}, f32[512,64]{0,1:T(8,128)S(1)}, u32[]{:S(2)}) copy-start(f32[512,64]{0,1:T(8,128)S(1)} %get-tuple-element.30) | copy-start | bytes 393220
  978.4 138.1 %copy-start.34 = (f32[1536]{0:T(1024)}, f32[1536]{0:T(1024)S(1)}, u32[]{:S(2)}) copy-start(f32[1536]{0:T(1024)S(1)} %fusion.80) | copy-start | bytes 18436
  1163.1 22.2 copy-start.4
  1240.0 19.2 copy-start.20
  1259.2 38.9 %copy-start.22 = (f32[3,16,512]{2,1,0:T(8,128)}, f32[3,16,512]{2,1,0:T(8,128)S(1)}, u32[]{:S(2)}) copy-start(f32[3,16,512]{2,1,0:T(8,128)S(1)} %fusion.23) | copy-start | bytes 294916
  1259.3 39.5 %copy-start.19 = (pred[512,512]{1,0:T(8,128)(4,1)S(1)}, pred[512,512]{1,0:T(8,128)(4,1)}, u32[]{:S(2)}) copy-start(pred[512,512]{1,0:T(8,128)(4,1)} %iota_compare_fusion) | copy-start | bytes 786436
  1298.8 49.9 %copy-start.2 = (bf16[3,512,16,64]{1,3,2,0:T(8,128)(2,1)S(1)}, bf16[3,512,16,64]{1,3,2,0:T(8,128)(2,1)}, u32[]{:S(2)}) copy-start(bf16[3,512,16,64]{1,3,2,0:T(8,128)(2,1)} %fusion.39) | copy-start | bytes 9437188
  1298.8 49.9 %copy-start.9 = (f32[512,64]{0,1:T(8,128)S(1)}, f32[512,64]{0,1:T(8,128)}, u32[]{:S(2)}) copy-start(f32[512,64]{0,1:T(8,128)} %copy-done.8) | copy-start | bytes 393220
  1407.4 33.3 %copy-start.1 = (bf16[3,512,16,128]{1,3,2,0:T(8,128)(2,1)S(1)}, bf16[3,512,16,128]{1,3,2,0:T(8,128)(2,1)}, u32[]{:S(2)}) copy-start(bf16[3,512,16,128]{1,3,2,0:T(8,128)(2,1)} %copy.59) | copy-start | bytes 18874372
  1484.0 19.9 slice-start.2
  1564.3 31.2 %copy-start.27 = (f32[1536]{0:T(1024)S(1)}, f32[1536]{0:T(1024)}, u32[]{:S(2)}) copy-start(f32[1536]{0:T(1024)} %copy-done.26) | copy-start | bytes 18436
  1607.7 864.5 %reduce-scatter.10.cloned.1.call-start = ((), (), s32[]{:S(2)}) async-start(), calls=%async_computation.12 | async-start | bytes 5308416 | tf_op jit(solution)/shard_map/reduce_scatter | solution.py:107
  1618.6 853.6 %reduce-scatter.12.cloned.1.call-start = ((), (), s32[]{:S(2)}) async-start(), calls=%async_computation.13 | async-start | bytes 9437184 | tf_op jit(solution)/shard_map/reduce_scatter | solution.py:107
  1633.8 838.4 %reduce-scatter.14.cloned.1.call-start = ((), (), s32[]{:S(2)}) async-start(), calls=%async_computation.14 | async-start | bytes 18874368 | tf_op jit(solution)/shard_map/reduce_scatter | solution.py:107
  1679.8 792.4 %reduce-scatter.8.cloned.1.call-start = ((), (), s32[]{:S(2)}) async-start(), calls=%async_computation.11 | async-start | bytes 28311552 | tf_op jit(solution)/shard_map/reduce_scatter | solution.py:107
  (33 other events, 278.8 us)
Sparse Core Ops, SparseCore 0:
  9.8 53.2 all-gather.13
  498.6 475.0 reduce-scatter.5
  975.6 68.2 all-gather.11
  1045.6 25.5 all-gather.7
  1072.8 32.8 all-gather.9
  1607.8 441.2 all-gather.15
  2053.1 48.0 reduce-scatter.9
  2105.2 65.8 reduce-scatter.11
  2175.2 110.5 reduce-scatter.13
  2289.8 150.6 reduce-scatter.7
where the time goes:
time: 2500 us; the launch traced here: 2480 us
  local copies, waits for them, and re-layouts  601 us (24%)
  other arithmetic  589 us (24%)
  waiting for transfers between devices  567 us (23%)
  matrix products  449 us (18%)
  blocking collectives  255 us (10%)
    gather x1, local copies, waits for them, and re-layouts, device_step(): picked = jnp.take(emb_table, jnp.where(is_owned, local_ids, 0), axis=0)  444 us
    scatter-add x3, other arithmetic, device_step(): jax.ops.segment_sum(all_grads, seg_ids, num_segments=vocab_dev)  380 us
    all_gather x1, waiting for transfers between devices, device_step(): all_grads = lax.all_gather(d_rows, 'fsdp', tiled=True)  283 us
    unnamed x2, blocking collectives  236 us
    reduce_scatter x1, waiting for transfers between devices, device_step(): tok_rows = lax.psum_scatter(picked, 'fsdp', scatter_dimension=0, tiled=True)  217 us
    dot_general x3, matrix products, attend_local(): jnp.einsum('bshd,bthd->bhst', q_proj[..., :NOPE_DIM], kv_up[..., :NOPE_DI...  120 us
    dot_general x3, matrix products, attend_local(): jnp.einsum('bhst,bthd->bshd', attn_probs, kv_up[..., NOPE_DIM:], preferre...  70.3 us
    all_gather x4, waiting for transfers between devices, device_step(): lax.all_gather(shard_piece, 'fsdp', tiled=True)  65.5 us
  transfers between devices with their start and end apart: 10, of which 3 were waited for; matrix products, arithmetic and copies ran while one was open for 47% of the time, Pallas kernels for 0%

commit v1 on v0

v1 whole, which is shorter than its diff:
```python
import math
import jax
import jax.numpy as jnp
from jax import lax
from jax.experimental import pallas as pl
from jax.experimental.pallas import tpu as pltpu
from jax.sharding import PartitionSpec as P

ALL, NEW = ..., None
ROW, COL, LAST = 0, 1, -1
TILE_ROWS, LANES, PAIR = 8, 128, 2
SMALL_FLOPS, LARGE_FLOPS, SOME_BYTES = 4 * 10**9, 2 * 10**10, 10**8
MUCH_VMEM, MOST_VMEM = 48 * 2**20, 60 * 2**20
NOPE_DIM = 128
ROPE_DIM = 64
VALUE_DIM = 128
ROPE_THETA = 50000.0
RMS_EPS = 1e-6
ATTN_SCALE = (NOPE_DIM + ROPE_DIM) ** -0.5 * (0.1 * math.log(32.0) + 1.0) ** 2
LOG2_E = math.log2(math.e)
ROW_DIMS = (((0,), (0,)), ((), ()))
COL_DIMS = (((1,), (1,)), ((), ()))
PAIR_DIM = 2 * (NOPE_DIM + ROPE_DIM)
HALF_ROPE = ROPE_DIM // 2
Q_ROWS = 256


def cost_of(flops):
    return pl.CostEstimate(flops=flops, bytes_accessed=SOME_BYTES, transcendentals=0)


def row_iota(shape):
    return lax.broadcasted_iota(jnp.int32, shape, ROW)


def col_iota(shape):
    return lax.broadcasted_iota(jnp.int32, shape, COL)


def rms_scale(in_vals, gain_vec):
    vals_f32 = in_vals.astype(jnp.float32)
    inv_rms = lax.rsqrt(jnp.mean(vals_f32 * vals_f32, axis=LAST, keepdims=True) + RMS_EPS)
    return (vals_f32 * inv_rms * gain_vec).astype(jnp.bfloat16)


def norm_back(rows_f32, d_normed, gain_vec):
    inv_rms = lax.rsqrt(jnp.mean(rows_f32 * rows_f32, axis=LAST, keepdims=True) + RMS_EPS)
    scaled = d_normed * gain_vec
    along = jnp.mean(scaled * rows_f32, axis=LAST, keepdims=True) * (inv_rms * inv_rms * inv_rms)
    return scaled * inv_rms - rows_f32 * along


def gain_back(rows_f32, d_normed):
    inv_rms = lax.rsqrt(jnp.mean(rows_f32 * rows_f32, axis=LAST, keepdims=True) + RMS_EPS)
    return jnp.sum(d_normed * (rows_f32 * inv_rms), axis=ROW)


def pair_source(width):
    at = jnp.arange(width)
    turned = at - 2 * NOPE_DIM
    part, head, i = turned // (2 * HALF_ROPE), lax.rem(turned // HALF_ROPE, PAIR), lax.rem(turned, HALF_ROPE)
    plain = (NOPE_DIM + ROPE_DIM) * (at // NOPE_DIM) + lax.rem(at, NOPE_DIM)
    return jnp.where(at < 2 * NOPE_DIM, plain, (NOPE_DIM + ROPE_DIM) * head + NOPE_DIM + HALF_ROPE * part + i)


def arrange_weights(w_query, w_down):
    rows, query_dim = w_query.shape
    kv_rank = w_down.shape[COL] - ROPE_DIM
    down_dim = kv_rank + 2 * ROPE_DIM
    pair_pick = (jnp.arange(PAIR_DIM)[:, NEW] == pair_source(PAIR_DIM)[NEW, :]).astype(w_query.dtype)
    twice = HALF_ROPE * (jnp.arange(2 * ROPE_DIM) // (2 * HALF_ROPE)) + lax.rem(jnp.arange(2 * ROPE_DIM), HALF_ROPE)
    twice_pick = (jnp.arange(ROPE_DIM)[:, NEW] == twice[NEW, :]).astype(w_query.dtype)

    def kernel(query_ref, down_ref, pair_ref, twice_ref, out_ref, low_ref):
        for at in range(0, query_dim, PAIR_DIM):
            out_ref[:, at:at + PAIR_DIM] = jnp.dot(query_ref[:, at:at + PAIR_DIM], pair_ref[ALL], preferred_element_type=jnp.float32).astype(out_ref.dtype)
        low_ref[:, :kv_rank] = down_ref[:, :kv_rank]
        low_ref[:, kv_rank:] = jnp.dot(down_ref[:, kv_rank:], twice_ref[ALL], preferred_element_type=jnp.float32).astype(low_ref.dtype)

    return pl.pallas_call(
        kernel,
        out_shape=(jax.ShapeDtypeStruct((rows, query_dim), w_query.dtype), jax.ShapeDtypeStruct((rows, down_dim), w_query.dtype)),
        in_specs=[pl.BlockSpec(memory_space=pltpu.VMEM)] * 4,
        out_specs=(pl.BlockSpec(memory_space=pltpu.VMEM),) * 2,
        cost_estimate=cost_of(SMALL_FLOPS),
        name='arrange_weights',
    )(w_query, w_down, pair_pick, twice_pick)


def head_columns(d_query_w):
    rows = d_query_w.shape[ROW]
    pairs = d_query_w.reshape(rows, -1, PAIR_DIM)
    plain = pairs[ALL, :2 * NOPE_DIM].reshape(rows, -1, 2, NOPE_DIM)
    rotary = pairs[ALL, 2 * NOPE_DIM:].reshape(rows, -1, 2, 2, HALF_ROPE)
    rotary = jnp.swapaxes(rotary, 2, 3).reshape(rows, -1, 2, ROPE_DIM)
    return jnp.concatenate([plain, rotary], axis=LAST).reshape(rows, -1)


def rope_tables(seq_len):
    positions = jnp.arange(seq_len, dtype=jnp.float32)
    inv_freq = ROPE_THETA ** (-2.0 * jnp.arange(HALF_ROPE, dtype=jnp.float32) / ROPE_DIM)
    rot_angle = positions[:, NEW] * inv_freq[NEW, :]
    cos_tab, sin_tab = jnp.cos(rot_angle), jnp.sin(rot_angle)
    return jnp.concatenate([cos_tab] * 4, axis=COL), jnp.concatenate([-sin_tab, -sin_tab, sin_tab, sin_tab], axis=COL)


def attend_pairs(q_all, kv_all, pe_all, d_mix, seq_count, side):
    tok_count = q_all.shape[ROW]
    seq_len = tok_count // seq_count
    n_pairs = q_all.shape[COL] // PAIR_DIM
    kv_dim = NOPE_DIM + VALUE_DIM
    cos_tab, sin_tab = rope_tables(seq_len)

    def kernel(side_s, q_ref, kv_ref, pe_ref, do_ref, cos_ref, sin_ref, mix_ref, own_ref, give_ref, dq_ref, dkv_ref, dpe_ref, key_acc):
        pair = pl.program_id(1)
        cos_vals, sin_vals = cos_ref[ALL], sin_ref[ALL]
        lane = col_iota((seq_len, 2 * ROPE_DIM))

        def turn(vals):
            return vals * cos_vals + pltpu.roll(vals, ROPE_DIM, 1) * sin_vals

        def turn_back(vals):
            return vals * cos_vals - pltpu.roll(vals, ROPE_DIM, 1) * sin_vals

        k_rot = turn(pe_ref[ALL].astype(jnp.float32)).astype(jnp.bfloat16)
        q_rot = turn(q_ref[:, 2 * NOPE_DIM:].astype(jnp.float32)).astype(jnp.bfloat16)
        n_blocks = seq_len // Q_ROWS
        d_q_rot = [None] * n_blocks
        d_k_rot = jnp.zeros((seq_len, 2 * ROPE_DIM), jnp.float32)
        in_head = [lax.rem(lane // HALF_ROPE, PAIR) == head for head in range(2)]
        keys = [jnp.concatenate([kv_ref[:, kv_dim * head:kv_dim * head + NOPE_DIM], jnp.where(in_head[head], k_rot, jnp.zeros_like(k_rot))], axis=COL) for head in range(2)]
        values = [kv_ref[:, kv_dim * head + NOPE_DIM:kv_dim * (head + 1)] for head in range(2)]
        queries = [jnp.concatenate([q_ref[:, NOPE_DIM * head:NOPE_DIM * (head + 1)], q_rot], axis=COL) for head in range(2)]
        d_out = [do_ref[:, VALUE_DIM * head:VALUE_DIM * (head + 1)] for head in range(2)]
        d_keys, d_values = {}, {}
        chains = [(head, block) for head in range(2) for block in range(n_blocks)]

        def first_dots(chain):
            head, block = chain
            rows, upto = slice(block * Q_ROWS, (block + 1) * Q_ROWS), (block + 1) * Q_ROWS
            scores = lax.dot_general(queries[head][rows], keys[head][:upto], COL_DIMS, preferred_element_type=jnp.float32)
            return scores, lax.dot_general(d_out[head][rows], values[head][:upto], COL_DIMS, preferred_element_type=jnp.float32)

        def softmax(chain, scores):
            _, block = chain
            row_at = block * Q_ROWS + row_iota(scores.shape)
            col_at = col_iota(scores.shape)
            scores = jnp.where(row_at >= col_at, scores, -1e30)
            powers = jnp.exp2((scores - jnp.max(scores, axis=LAST, keepdims=True)) * (ATTN_SCALE * LOG2_E))
            return powers * (1.0 / jnp.sum(powers, axis=LAST, keepdims=True))

        def last_dots(chain, probs, d_probs):
            head, block = chain
            rows, upto = slice(block * Q_ROWS, (block + 1) * Q_ROWS), (block + 1) * Q_ROWS
            probs_low = probs.astype(jnp.bfloat16)
            mixed = jnp.dot(probs_low, values[head][:upto], preferred_element_type=jnp.float32)
            mix_ref[rows, VALUE_DIM * head:VALUE_DIM * (head + 1)] = mixed.astype(jnp.bfloat16)
            leaning = jnp.sum(mixed * d_out[head][rows].astype(jnp.float32), axis=LAST, keepdims=True)
            d_scores = (probs * (d_probs - leaning)).astype(jnp.bfloat16)
            d_queries = jnp.dot(d_scores, keys[head][:upto], preferred_element_type=jnp.float32) * ATTN_SCALE
            dq_ref[rows, NOPE_DIM * head:NOPE_DIM * (head + 1)] = d_queries[:, :NOPE_DIM].astype(jnp.bfloat16)
            d_q_rot[block] = d_queries[:, NOPE_DIM:] if d_q_rot[block] is None else d_q_rot[block] + d_queries[:, NOPE_DIM:]
            key_part = lax.dot_general(d_scores, queries[head][rows], ROW_DIMS, preferred_element_type=jnp.float32)
            value_part = lax.dot_general(probs_low, d_out[head][rows], ROW_DIMS, preferred_element_type=jnp.float32)
            for below in range(block + 1):
                cut = slice(below * Q_ROWS, (below + 1) * Q_ROWS)
                for have, part in ((d_keys, key_part), (d_values, value_part)):
                    have[head, below] = have[head, below] + part[cut] if (head, below) in have else part[cut]

        ready = first_dots(chains[0])
        held = None
        for at, chain in enumerate(chains):
            scores, d_probs = ready
            if at + 1 < len(chains):
                ready = first_dots(chains[at + 1])
            if held is not None:
                last_dots(*held)
            held = (chain, softmax(chain, scores), d_probs)
        last_dots(*held)
        for head in range(2):
            all_keys = jnp.concatenate([d_keys[head, below] for below in range(n_blocks)], axis=ROW) * ATTN_SCALE
            dkv_ref[:, kv_dim * head:kv_dim * head + NOPE_DIM] = all_keys[:, :NOPE_DIM].astype(jnp.bfloat16)
            dkv_ref[:, kv_dim * head + NOPE_DIM:kv_dim * (head + 1)] = jnp.concatenate([d_values[head, below] for below in range(n_blocks)], axis=ROW).astype(jnp.bfloat16)
            d_k_rot = d_k_rot + jnp.where(in_head[head], all_keys[:, NOPE_DIM:], 0.0)
        dq_ref[:, 2 * NOPE_DIM:] = turn_back(jnp.concatenate(d_q_rot, axis=ROW)).astype(jnp.bfloat16)

        is_own = lax.rem(pair, PAIR) == side_s[0]

        @pl.when(is_own)
        def _():
            own_ref[ALL] = mix_ref[ALL]

        @pl.when(jnp.logical_not(is_own))
        def _():
            give_ref[ALL] = mix_ref[ALL]

        @pl.when(pair == 0)
        def _():
            key_acc[ALL] = d_k_rot

        @pl.when(pair > 0)
        def _():
            key_acc[ALL] += d_k_rot

        @pl.when(pair == n_pairs - 1)
        def _():
            both = key_acc[ALL]
            both = both + pltpu.roll(both, 2 * ROPE_DIM - HALF_ROPE, 1)
            both = jnp.where(lax.rem(lane // HALF_ROPE, PAIR) == 0, turn_back(both), 0.0)
            dpe_ref[ALL] = both.astype(jnp.bfloat16)

    def pair_block(width):
        return pl.BlockSpec((seq_len, width), lambda seq, pair, side: (seq, pair))

    half_block = pl.BlockSpec((seq_len, 2 * VALUE_DIM), lambda seq, pair, side: (seq, pair // 2))
    seq_block = pl.BlockSpec((seq_len, 2 * ROPE_DIM), lambda seq, pair, side: (seq, 0))
    tab_block = pl.BlockSpec((seq_len, 2 * ROPE_DIM), lambda seq, pair, side: (0, 0))
    shape = lambda width: jax.ShapeDtypeStruct((tok_count, width), jnp.bfloat16)
    return pl.pallas_call(
        kernel,
        grid_spec=pltpu.PrefetchScalarGridSpec(
            num_scalar_prefetch=1,
            grid=(seq_count, n_pairs),
            in_specs=[pair_block(PAIR_DIM), pair_block(2 * kv_dim), seq_block, pair_block(2 * VALUE_DIM), tab_block, tab_block],
            out_specs=(pair_block(2 * VALUE_DIM), half_block, half_block, pair_block(PAIR_DIM), pair_block(2 * kv_dim), seq_block),
            scratch_shapes=[pltpu.VMEM((seq_len, 2 * ROPE_DIM), jnp.float32)],
        ),
        out_shape=(shape(n_pairs * 2 * VALUE_DIM), shape(n_pairs * VALUE_DIM), shape(n_pairs * VALUE_DIM), shape(n_pairs * PAIR_DIM), shape(n_pairs * 2 * kv_dim), shape(2 * ROPE_DIM)),
        compiler_params=pltpu.CompilerParams(vmem_limit_bytes=MUCH_VMEM),
        cost_estimate=cost_of(LARGE_FLOPS),
        name='attend_pairs',
    )(side.reshape(1), q_all, kv_all, pe_all, d_mix, cos_tab, sin_tab)


BASE_CAP = 144
HEAVY_CAP = 480
RELAY_ROWS = 240
RELAY_PARTS = 3
DEST_ROWS = BASE_CAP + HEAVY_CAP
GROUP_ROWS = 48
FETCH_SLOTS = 6
TABLE_SLOTS = 4
SLOT_TILE = 136
MIX_TILE = 256
OUT_ROWS = 128
STEP_ROWS = 128
MESH_ID = pl.DeviceIdType.MESH


def shifted_sum(counts):
    size = counts.shape[LAST]
    lower = jnp.arange(size)[:, NEW] < jnp.arange(size)[NEW, :]
    return jnp.sum(jnp.where(lower, counts[ALL, :, None], 0), axis=-2)


def owner_cap(owner):
    return BASE_CAP + jnp.where(owner == 0, HEAVY_CAP, 0)


def plan_ids(flat_ids, vocab_dev, n_dev):
    order = jnp.arange(flat_ids.shape[ROW])
    same_before = (flat_ids[:, NEW] == flat_ids[NEW, :]) & (order[:, NEW] < order[NEW, :])
    is_first = jnp.logical_not(jnp.any(same_before, axis=ROW))
    lower = (flat_ids[:, NEW] < flat_ids[NEW, :]) & is_first[:, NEW]
    unique_rank = jnp.sum(lower.astype(jnp.int32), axis=ROW)
    owner = flat_ids // vocab_dev
    owned = owner[:, NEW] == jnp.arange(n_dev)[NEW, :]
    counts = jnp.sum((owned & is_first[:, NEW]).astype(jnp.int32), axis=ROW)
    owner_rank = unique_rank - jnp.sum(jnp.where(owned, shifted_sum(counts)[NEW, :], 0), axis=COL)
    return owner, owner_rank, is_first, counts


def slots_of(owner, owner_rank, dev, n_dev, turn):
    cap = owner_cap(owner)
    within = owner_rank - turn * cap
    slot = jnp.where(within < BASE_CAP, BASE_CAP * (owner ^ dev) + within, BASE_CAP * (n_dev - 1) + within)
    return jnp.where((within >= 0) & (within < cap), slot, -1)


def slot_list(flat_ids, slot_of, is_first, n_slots):
    hits = (slot_of[:, NEW] == jnp.arange(n_slots)[NEW, :]) & is_first[:, NEW]
    return jnp.sum(jnp.where(hits, flat_ids[:, NEW] + 1, 0), axis=ROW) - 1


def wanted_lists(all_slots, my_dev, n_dev):
    hop = jnp.arange(n_dev)[:, NEW] ^ my_dev
    base = all_slots[:, :n_dev * BASE_CAP].reshape(n_dev, n_dev, BASE_CAP)
    base = jnp.sum(jnp.where((hop == jnp.arange(n_dev)[NEW, :])[:, :, NEW], base, 0), axis=COL)
    heavy = jnp.where(my_dev == 0, all_slots[:, n_dev * BASE_CAP:], -1)
    by_dest = jnp.concatenate([base, heavy], axis=COL)
    return jnp.sum(jnp.where((hop == jnp.arange(n_dev)[NEW, :])[:, :, NEW], by_dest[:, NEW, :], 0), axis=ROW)


def pick_rows(table, lists, my_dev):
    vocab_dev, width = table.shape
    n_dev = lists.shape[ROW]
    flat = lists.reshape(-1)
    at = jnp.arange(n_dev * DEST_ROWS)
    local = jnp.where(flat < 0, lax.rem(TILE_ROWS * at, vocab_dev), jnp.clip(flat - my_dev * vocab_dev, 0, vocab_dev - 1))
    tiles = TILE_ROWS * (local // TILE_ROWS)
    tags = lax.rem(local, TILE_ROWS) + TILE_ROWS * lax.rem(at, GROUP_ROWS)
    tags = jnp.broadcast_to(tags[:, NEW], (n_dev * DEST_ROWS, LANES))
    all_groups = DEST_ROWS // GROUP_ROWS
    few_groups = -(-BASE_CAP // GROUP_ROWS)

    def kernel(tiles_s, dev_s, table_ref, tags_ref, out_ref, fetched, named, picked, fetch_sem, name_sem, out_sem):
        per_dest = jnp.where(dev_s[0] == 0, all_groups, few_groups)
        n_groups = n_dev * per_dest

        def row_at(group):
            dest = group // per_dest
            return pl.multiple_of(dest * DEST_ROWS + GROUP_ROWS * (group - dest * per_dest), GROUP_ROWS)

        def start_fetch(group):
            slot = lax.rem(group, FETCH_SLOTS)
            row = row_at(jnp.minimum(group, n_groups - 1))
            pltpu.make_async_copy(tags_ref.at[pl.ds(row, GROUP_ROWS)], named.at[slot], name_sem.at[slot]).start()
            for i in range(GROUP_ROWS):
                pltpu.make_async_copy(table_ref.at[pl.ds(pl.multiple_of(tiles_s[row + i], TILE_ROWS), TILE_ROWS)], fetched.at[slot, pl.ds(TILE_ROWS * i, TILE_ROWS)], fetch_sem.at[slot]).start()

        def wait_fetch(slot):
            pltpu.make_async_copy(named.at[slot], named.at[slot], name_sem.at[slot]).wait()
            pltpu.make_async_copy(fetched.at[slot], fetched.at[slot], fetch_sem.at[slot]).wait()

        def out_copy(group):
            slot = lax.rem(group, TABLE_SLOTS)
            return pltpu.make_async_copy(picked.at[slot], out_ref.at[pl.ds(row_at(group), GROUP_ROWS)], out_sem.at[slot])

        for ahead in range(FETCH_SLOTS - 1):
            start_fetch(jnp.int32(ahead))

        def body(group, carry):
            @pl.when(group >= TABLE_SLOTS)
            def _():
                out_copy(group - TABLE_SLOTS).wait()

            slot = lax.rem(group, FETCH_SLOTS)
            wait_fetch(slot)
            start_fetch(group + FETCH_SLOTS - 1)
            lane = col_iota((GROUP_ROWS, LANES))
            name = named[slot]
            chooser = jnp.concatenate([(name == lane + at).astype(jnp.float32) for at in range(0, TILE_ROWS * GROUP_ROWS, LANES)], axis=COL).astype(jnp.bfloat16)
            picked[lax.rem(group, TABLE_SLOTS)] = jnp.dot(chooser, fetched[slot], preferred_element_type=jnp.float32).astype(jnp.bfloat16)
            out_copy(group).start()
            return carry

        lax.fori_loop(0, n_groups, body, 0)
        for ahead in range(FETCH_SLOTS - 1):
            wait_fetch(lax.rem(n_groups + ahead, FETCH_SLOTS))
        for back in range(TABLE_SLOTS, 0, -1):
            out_copy(n_groups - back).wait()

    return pl.pallas_call(
        kernel,
        out_shape=jax.ShapeDtypeStruct((n_dev * DEST_ROWS, width), table.dtype),
        grid_spec=pltpu.PrefetchScalarGridSpec(
            num_scalar_prefetch=2,
            grid=(1,),
            in_specs=[pl.BlockSpec(memory_space=pl.ANY)] * 2,
            out_specs=pl.BlockSpec(memory_space=pl.ANY),
            scratch_shapes=[
                pltpu.VMEM((FETCH_SLOTS, TILE_ROWS * GROUP_ROWS, width), table.dtype),
                pltpu.VMEM((FETCH_SLOTS, GROUP_ROWS, LANES), jnp.int32),
                pltpu.VMEM((TABLE_SLOTS, GROUP_ROWS, width), table.dtype),
                pltpu.SemaphoreType.DMA((FETCH_SLOTS,)),
                pltpu.SemaphoreType.DMA((FETCH_SLOTS,)),
                pltpu.SemaphoreType.DMA((TABLE_SLOTS,)),
            ],
        ),
        cost_estimate=cost_of(SMALL_FLOPS),
        name='pick_rows',
    )(tiles, my_dev.reshape(1), table, tags)


def greet_all(my_dev, n_dev):
    barrier = pltpu.get_barrier_semaphore()
    for hop in range(1, n_dev):
        pl.semaphore_signal(barrier, inc=1, device_id={'fsdp': my_dev ^ hop}, device_id_type=MESH_ID)
    pl.semaphore_wait(barrier, n_dev - 1)


def remote(source, target, send_sem, recv_sem, dest):
    return pltpu.make_async_remote_copy(src_ref=source, dst_ref=target, send_sem=send_sem, recv_sem=recv_sem, device_id={'fsdp': dest}, device_id_type=MESH_ID)


def swap_rows(picked, n_dev, work=None):
    width = picked.shape[LAST]
    n_slots = n_dev * BASE_CAP + HEAVY_CAP
    n_tiles = n_slots // SLOT_TILE
    tok_count = 0 if work is None else work[1].shape[ROW]
    heavy_at = n_dev * BASE_CAP
    part_rows = RELAY_ROWS // RELAY_PARTS

    def kernel(*refs):
        if work is None:
            in_ref, out_ref, relay_ref, local, send_sem, recv_sem, relay_send, relay_recv, local_sem = refs
        else:
            in_ref, at_ref, dy_ref, w_out_ref, out_ref, relay_ref, sums_ref, mix_ref, local, send_sem, recv_sem, relay_send, relay_recv, local_sem, dy_vals, w_vals, sums, mixes, load_sem, store_sem = refs
        my_dev = lax.axis_index('fsdp')
        greet_all(my_dev, n_dev)

        def base_copy(hop):
            return remote(in_ref.at[pl.ds(hop * DEST_ROWS, BASE_CAP)], out_ref.at[pl.ds(hop * BASE_CAP, BASE_CAP)], send_sem.at[hop], recv_sem.at[hop], my_dev ^ hop)

        def heavy_copy(dest):
            rows = HEAVY_CAP - (RELAY_ROWS if dest >= 6 else 0)
            return remote(in_ref.at[pl.ds(dest * DEST_ROWS + BASE_CAP, rows)], out_ref.at[pl.ds(heavy_at, rows)], send_sem.at[7 + dest], recv_sem.at[8], jnp.int32(dest))

        def relay_in(dest, part):
            at = dest * DEST_ROWS + DEST_ROWS - RELAY_ROWS + part * part_rows
            return remote(in_ref.at[pl.ds(at, part_rows)], relay_ref.at[pl.ds(part * part_rows, part_rows)], relay_send.at[dest - 6, part], relay_recv.at[part], jnp.int32(dest - 2))

        def relay_out(dest, part):
            at = heavy_at + HEAVY_CAP - RELAY_ROWS + part * part_rows
            return remote(relay_ref.at[pl.ds(part * part_rows, part_rows)], out_ref.at[pl.ds(at, part_rows)], relay_send.at[0, part], relay_recv.at[part], jnp.int32(dest))

        @pl.when(my_dev == 0)
        def _():
            for part in range(RELAY_PARTS):
                for dest in (6, 7):
                    relay_in(dest, part).start()
            for dest in (6, 7, 2, 4, 3, 5, 1):
                heavy_copy(dest).start()

        for hop in (6, 7, 2, 4, 3, 5, 1):
            base_copy(hop).start()
        if work is not None:
            loads = (pltpu.make_async_copy(dy_ref, dy_vals, load_sem.at[0]), pltpu.make_async_copy(w_out_ref, w_vals, load_sem.at[1]))
            for load in loads:
                load.start()
        own = pltpu.make_async_copy(in_ref.at[pl.ds(0, DEST_ROWS)], local, local_sem.at[0])
        own.start()
        own.wait()
        back = pltpu.make_async_copy(local.at[pl.ds(0, BASE_CAP)], out_ref.at[pl.ds(0, BASE_CAP)], local_sem.at[1])
        back.start()

        @pl.when(my_dev == 0)
        def _():
            mine = pltpu.make_async_copy(local.at[pl.ds(BASE_CAP, HEAVY_CAP)], out_ref.at[pl.ds(heavy_at, HEAVY_CAP)], local_sem.at[2])
            mine.start()
            mine.wait()

        back.wait()
        if work is not None:
            def sums_copy(tile):
                return pltpu.make_async_copy(sums.at[lax.rem(tile, PAIR)], sums_ref.at[pl.ds(pl.multiple_of(tile * SLOT_TILE, TILE_ROWS), SLOT_TILE)], store_sem.at[lax.rem(tile, PAIR)])

            def mix_copy(tile):
                return pltpu.make_async_copy(mixes.at[lax.rem(tile, PAIR)], mix_ref.at[pl.ds(pl.multiple_of(tile * MIX_TILE, TILE_ROWS), MIX_TILE)], store_sem.at[2 + lax.rem(tile, PAIR)])

            def sum_tile(tile, carry):
                @pl.when(tile >= 2)
                def _():
                    sums_copy(tile - 2).wait()

                slot = tile * SLOT_TILE + row_iota((SLOT_TILE, tok_count))
                chooser = (slot == at_ref[ALL]).astype(jnp.float32).astype(jnp.bfloat16)
                sums[lax.rem(tile, PAIR)] = jnp.dot(chooser, dy_vals[ALL], preferred_element_type=jnp.float32)
                sums_copy(tile).start()
                return carry

            def mix_tile(tile, carry):
                @pl.when(tile >= 2)
                def _():
                    mix_copy(tile - 2).wait()

                rows = dy_vals[pl.ds(pl.multiple_of(tile * MIX_TILE, MIX_TILE), MIX_TILE)]
                mixes[lax.rem(tile, PAIR)] = lax.dot_general(rows, w_vals[ALL], COL_DIMS, preferred_element_type=jnp.float32).astype(jnp.bfloat16)
                mix_copy(tile).start()
                return carry

            loads[0].wait()
            lax.fori_loop(0, n_tiles, sum_tile, 0)
        for mid in (4, 5):
            @pl.when(my_dev == mid)
            def _(mid=mid):
                for part in range(RELAY_PARTS):
                    relay_in(mid + 2, part).wait_recv()
                    relay_out(mid + 2, part).start()
                for part in range(RELAY_PARTS):
                    relay_out(mid + 2, part).wait_send()
        if work is not None:
            loads[1].wait()
            lax.fori_loop(0, tok_count // MIX_TILE, mix_tile, 0)
            for back_at in (2, 1):
                sums_copy(jnp.int32(n_tiles - back_at)).wait()
                mix_copy(jnp.int32(tok_count // MIX_TILE - back_at)).wait()
        for hop in range(1, n_dev):
            base_copy(hop).wait()
        for dest in range(1, n_dev):
            @pl.when(my_dev == dest)
            def _(dest=dest):
                heavy_copy(dest).wait_recv()
                if dest >= 6:
                    for part in range(RELAY_PARTS):
                        relay_out(dest, part).wait_recv()

            @pl.when(my_dev == 0)
            def _(dest=dest):
                heavy_copy(dest).wait_send()
                if dest >= 6:
                    for part in range(RELAY_PARTS):
                        relay_in(dest, part).wait_send()

    any_spec = pl.BlockSpec(memory_space=pl.ANY)
    out_shape = [jax.ShapeDtypeStruct((n_slots, width), picked.dtype), jax.ShapeDtypeStruct((RELAY_ROWS, width), picked.dtype)]
    in_specs = [any_spec]
    scratch_shapes = [
        pltpu.VMEM((DEST_ROWS, width), picked.dtype),
        pltpu.SemaphoreType.DMA((15,)),
        pltpu.SemaphoreType.DMA((9,)),
        pltpu.SemaphoreType.DMA((2, RELAY_PARTS)),
        pltpu.SemaphoreType.DMA((RELAY_PARTS,)),
        pltpu.SemaphoreType.DMA((3,)),
    ]
    if work is not None:
        in_specs += [pl.BlockSpec(memory_space=pltpu.VMEM), any_spec, any_spec]
        out_shape += [jax.ShapeDtypeStruct((n_slots, width), jnp.float32), jax.ShapeDtypeStruct((tok_count, work[2].shape[ROW]), jnp.bfloat16)]
        scratch_shapes += [
            pltpu.VMEM(work[1].shape, work[1].dtype),
            pltpu.VMEM(work[2].shape, work[2].dtype),
            pltpu.VMEM((2, SLOT_TILE, width), jnp.float32),
            pltpu.VMEM((2, MIX_TILE, work[2].shape[ROW]), jnp.bfloat16),
            pltpu.SemaphoreType.DMA((2,)),
            pltpu.SemaphoreType.DMA((4,)),
        ]
    outs = pl.pallas_call(
        kernel,
        out_shape=tuple(out_shape),
        in_specs=in_specs,
        out_specs=(any_spec,) * len(out_shape),
        scratch_shapes=scratch_shapes,
        compiler_params=pltpu.CompilerParams(collective_id=1 if work is None else 3, has_side_effects=True, vmem_limit_bytes=MUCH_VMEM),
        cost_estimate=cost_of(LARGE_FLOPS),
        name='swap_rows',
    )(picked, *(work or ()))
    return outs[0] if work is None else (outs[0], outs[2], outs[3])


def table_parts(source):
    if source < 6:
        return ((0, BASE_CAP), (BASE_CAP, HEAVY_CAP))
    return ((0, BASE_CAP), (BASE_CAP, HEAVY_CAP - RELAY_ROWS), (DEST_ROWS - RELAY_ROWS, RELAY_ROWS))


def permute_rows(parts, n_dev):
    base, direct, relayed = parts[:n_dev], parts[n_dev], parts[n_dev + 1]
    heavy = jnp.concatenate([direct, relayed], axis=ROW)
    passed = lax.ppermute(relayed, 'fsdp', [(6, 2), (7, 3)])
    arrived = {0: [heavy]}
    for source in (6, 7):
        arrived[source] = [lax.ppermute(direct, 'fsdp', [(source, 0)])]
    for source in (2, 4, 3, 5, 1):
        arrived[source] = [lax.ppermute(heavy, 'fsdp', [(source, 0)])]
    for source in (6, 7):
        arrived[source].append(lax.ppermute(passed, 'fsdp', [(source - 4, 0)]))
    base = [base[0]] + [lax.ppermute(base[hop], 'fsdp', [(dev, dev ^ hop) for dev in range(n_dev)]) for hop in range(1, n_dev)]
    return [piece for source in range(n_dev) for piece in [base[source]] + arrived[source]]


def return_rows(slot_grads, n_dev):
    width = slot_grads.shape[LAST]
    heavy_at = n_dev * BASE_CAP

    def kernel(in_ref, out_ref, local, send_sem, recv_sem, local_sem):
        my_dev = lax.axis_index('fsdp')
        greet_all(my_dev, n_dev)

        def base_copy(hop):
            place = pl.ds(hop * BASE_CAP, BASE_CAP)
            return remote(in_ref.at[place], out_ref.at[place], send_sem.at[hop], recv_sem.at[hop], my_dev ^ hop)

        def heavy_copy(source):
            return remote(in_ref.at[pl.ds(heavy_at, HEAVY_CAP)], out_ref.at[pl.ds(heavy_at + source * HEAVY_CAP, HEAVY_CAP)], send_sem.at[8], recv_sem.at[7 + source], jnp.int32(0))

        for source in range(1, n_dev):
            @pl.when(my_dev == source)
            def _(source=source):
                heavy_copy(source).start()
        for hop in range(1, n_dev):
            base_copy(hop).start()

        def bounce(at, rows):
            for one in (pltpu.make_async_copy(in_ref.at[pl.ds(at, rows)], local.at[pl.ds(0, rows)], local_sem), pltpu.make_async_copy(local.at[pl.ds(0, rows)], out_ref.at[pl.ds(at, rows)], local_sem)):
                one.start()
                one.wait()

        bounce(0, BASE_CAP)

        @pl.when(my_dev == 0)
        def _():
            bounce(heavy_at, HEAVY_CAP)

        for hop in range(1, n_dev):
            base_copy(hop).wait()
        for source in range(1, n_dev):
            @pl.when(my_dev == source)
            def _(source=source):
                heavy_copy(source).wait_send()

            @pl.when(my_dev == 0)
            def _(source=source):
                heavy_copy(source).wait_recv()

    arrived = pl.pallas_call(
        kernel,
        out_shape=jax.ShapeDtypeStruct((n_dev * DEST_ROWS, width), slot_grads.dtype),
        in_specs=[pl.BlockSpec(memory_space=pl.ANY)],
        out_specs=pl.BlockSpec(memory_space=pl.ANY),
        scratch_shapes=[
            pltpu.VMEM((HEAVY_CAP, width), slot_grads.dtype),
            pltpu.SemaphoreType.DMA((9,)),
            pltpu.SemaphoreType.DMA((15,)),
            pltpu.SemaphoreType.DMA,
        ],
        compiler_params=pltpu.CompilerParams(collective_id=2, has_side_effects=True),
        cost_estimate=cost_of(SMALL_FLOPS),
        name='return_rows',
    )(slot_grads)
    pieces = []
    for source in range(n_dev):
        pieces.append(arrived[source * BASE_CAP:(source + 1) * BASE_CAP])
        heavy_part = arrived[heavy_at + source * HEAVY_CAP:heavy_at + (source + 1) * HEAVY_CAP]
        pieces += [heavy_part[start - BASE_CAP:start - BASE_CAP + rows] for start, rows in table_parts(source)[1:]]
    return pieces


def table_plan(lists, my_dev, vocab_dev):
    n_dev = lists.shape[ROW]
    n_out = vocab_dev // OUT_ROWS
    edges = my_dev * vocab_dev + OUT_ROWS * jnp.arange(n_out + 1)
    below = (lists[NEW, :, :] >= 0) & (lists[NEW, :, :] < edges[:, NEW, NEW])
    upto = jnp.sum(below.astype(jnp.int32), axis=LAST)
    low, high = upto[:-1], upto[1:]
    firsts = low // TILE_ROWS
    counts = jnp.where(high > low, (high + 7) // TILE_ROWS - firsts, 0)
    names = jnp.broadcast_to(lists.reshape(-1, 1), (n_dev * DEST_ROWS, LANES))
    return firsts.reshape(-1), counts.reshape(-1), names


def write_table(pieces, plan, my_dev, vocab_dev, out_dtype, so_far=None):
    firsts, counts, names = plan
    width = pieces[0].shape[LAST]
    n_out = vocab_dev // OUT_ROWS
    n_part = len(pieces)
    n_source = firsts.shape[ROW] // n_out
    tile_blocks = OUT_ROWS // TILE_ROWS
    cap_rows = TILE_ROWS * n_source * (tile_blocks + 1)
    cap_rows = -(-cap_rows // STEP_ROWS) * STEP_ROWS

    def kernel(firsts_s, counts_s, dev_s, *refs):
        part_refs, names_ref = refs[:n_part], refs[n_part]
        old_ref = refs[n_part + 1] if so_far is not None else None
        out_ref, staged, named, total, ready, filled_s, row_sem, out_sem, old_sem = refs[-9:]

        def start_fetch(block):
            slot = lax.rem(block, TABLE_SLOTS)
            where = jnp.int32(0)
            first_ref = 0
            for source in range(n_source):
                parts = table_parts(source)
                first = firsts_s[block * n_source + source]

                def one(i, at, parts=parts, source=source, first=first, first_ref=first_ref):
                    block_at = first + i
                    place = pl.ds(pl.multiple_of(TILE_ROWS * at, TILE_ROWS), TILE_ROWS)
                    named[slot, place] = names_ref[pl.ds(pl.multiple_of(source * DEST_ROWS + TILE_ROWS * block_at, TILE_ROWS), TILE_ROWS)]
                    for part, (start, rows) in enumerate(parts):
                        @pl.when((block_at >= start // TILE_ROWS) & (block_at < (start + rows) // TILE_ROWS))
                        def _(part=part, start=start):
                            pltpu.make_async_copy(part_refs[first_ref + part].at[pl.ds(pl.multiple_of(TILE_ROWS * block_at - start, TILE_ROWS), TILE_ROWS)], staged.at[slot, place], row_sem.at[slot]).start()
                    return at + 1

                where = lax.fori_loop(0, counts_s[block * n_source + source], one, where)
                first_ref += len(parts)
            filled_s[slot] = where

        def out_copy(block):
            slot = lax.rem(block, TABLE_SLOTS)
            return pltpu.make_async_copy(ready.at[slot], out_ref.at[pl.ds(pl.multiple_of(block * OUT_ROWS, OUT_ROWS), OUT_ROWS)], out_sem.at[slot])

        for ahead in range(TABLE_SLOTS - 1):
            start_fetch(jnp.int32(ahead))

        def body(out_block, carry):
            @pl.when(out_block + TABLE_SLOTS - 1 < n_out)
            def _():
                start_fetch(out_block + TABLE_SLOTS - 1)

            @pl.when(out_block >= TABLE_SLOTS)
            def _():
                out_copy(out_block - TABLE_SLOTS).wait()

            slot = lax.rem(out_block, TABLE_SLOTS)
            n_blocks = filled_s[slot]

            def wait_one(i, carry):
                pltpu.make_async_copy(staged.at[slot, pl.ds(0, TILE_ROWS)], staged.at[slot, pl.ds(0, TILE_ROWS)], row_sem.at[slot]).wait()
                return carry

            lax.fori_loop(0, n_blocks, wait_one, 0)
            low_row = dev_s[0] * vocab_dev + out_block * OUT_ROWS

            def summed(start, rows, store):
                place = pl.ds(start, rows)
                live = start + row_iota((rows, OUT_ROWS)) < TILE_ROWS * n_blocks
                lane = col_iota((rows, OUT_ROWS))
                chooser = ((named[slot, place] - low_row == lane) & live).astype(jnp.float32)
                chooser = jnp.concatenate([chooser] * 3, axis=ROW).T.astype(jnp.bfloat16)
                for col in range(0, width, 512):
                    part = jnp.where(live[:, :1], staged[slot, place, col:col + 512], 0.0)
                    high = part.astype(jnp.bfloat16)
                    left = part - high.astype(jnp.float32)
                    mid = left.astype(jnp.bfloat16)
                    low = (left - mid.astype(jnp.float32)).astype(jnp.bfloat16)
                    stacked = jnp.concatenate([high, mid, low], axis=ROW)
                    store(col, jnp.dot(chooser, stacked, preferred_element_type=jnp.float32))

            def store_out(col, vals):
                ready[slot, :, col:col + 512] = vals.astype(out_dtype)

            def store_more(col, vals):
                total[:, col:col + 512] += vals

            few = jnp.int32(-1) if so_far is not None else n_blocks

            @pl.when(few == 0)
            def _():
                ready[slot] = jnp.zeros((OUT_ROWS, width), out_dtype)

            @pl.when((few > 0) & (few <= STEP_ROWS // 16))
            def _():
                summed(0, STEP_ROWS // 2, store_out)

            @pl.when((few > STEP_ROWS // 16) & (few <= STEP_ROWS // TILE_ROWS))
            def _():
                summed(0, STEP_ROWS, store_out)

            @pl.when((few < 0) | (few > STEP_ROWS // TILE_ROWS))
            def _():
                if so_far is None:
                    total[ALL] = jnp.zeros_like(total)
                else:
                    old = pltpu.make_async_copy(old_ref.at[pl.ds(pl.multiple_of(out_block * OUT_ROWS, OUT_ROWS), OUT_ROWS)], total, old_sem)
                    old.start()
                    old.wait()

                def add_step(step, carry):
                    summed(pl.multiple_of(step * STEP_ROWS, STEP_ROWS), STEP_ROWS, store_more)
                    return carry

                lax.fori_loop(0, (TILE_ROWS * n_blocks + STEP_ROWS - 1) // STEP_ROWS, add_step, 0)
                ready[slot] = total[ALL].astype(out_dtype)

            out_copy(out_block).start()
            return carry

        lax.fori_loop(0, n_out, body, 0)
        for back in range(TABLE_SLOTS, 0, -1):
            out_copy(n_out - back).wait()

    extra = () if so_far is None else (so_far,)
    any_spec = pl.BlockSpec(memory_space=pl.ANY)
    return pl.pallas_call(
        kernel,
        out_shape=jax.ShapeDtypeStruct((vocab_dev, width), out_dtype),
        grid_spec=pltpu.PrefetchScalarGridSpec(
            num_scalar_prefetch=3,
            grid=(1,),
            in_specs=[any_spec] * n_part + [pl.BlockSpec(names.shape, lambda i, *_: (0, 0))] + [any_spec] * len(extra),
            out_specs=any_spec,
            scratch_shapes=[
                pltpu.VMEM((TABLE_SLOTS, cap_rows, width), jnp.float32),
                pltpu.VMEM((TABLE_SLOTS, cap_rows, LANES), jnp.int32),
                pltpu.VMEM((OUT_ROWS, width), jnp.float32),
                pltpu.VMEM((TABLE_SLOTS, OUT_ROWS, width), out_dtype),
                pltpu.SMEM((TABLE_SLOTS,), jnp.int32),
                pltpu.SemaphoreType.DMA((TABLE_SLOTS,)),
                pltpu.SemaphoreType.DMA((TABLE_SLOTS,)),
                pltpu.SemaphoreType.DMA,
            ],
        ),
        compiler_params=pltpu.CompilerParams(vmem_limit_bytes=MOST_VMEM),
        cost_estimate=cost_of(SMALL_FLOPS),
        name='write_table',
    )(firsts, counts, my_dev.reshape(1), *pieces, names, *extra)


GRAD_TILE = 512
NORM_ROWS = 256


def after(vals, *deps):
    return lax.optimization_barrier((vals,) + deps)[0]


def side_blocks(rows, side, n_dev):
    block = rows.shape[COL] // n_dev
    cuts = [rows[:, at * block:(at + 1) * block] for at in range(n_dev)]
    even, odd = jnp.concatenate(cuts[0::2], axis=COL), jnp.concatenate(cuts[1::2], axis=COL)
    return jnp.where(side == 0, even, odd), jnp.where(side == 0, odd, even)


def expand_rows(slot_of, slot_rows, gain_f32, side, n_dev):
    n_slots, width = slot_rows.shape
    tok_count = slot_of.shape[ROW]
    slot_cols = jnp.broadcast_to(slot_of[:, NEW], (tok_count, LANES))

    def kernel(side_s, at_ref, rows_ref, gain_ref, tok_ref, norm_ref, own_ref, give_ref):
        lane = col_iota((NORM_ROWS, n_slots))
        chooser = (at_ref[:, :1] == lane).astype(jnp.float32).astype(jnp.bfloat16)
        vals = jnp.dot(chooser, rows_ref[ALL], preferred_element_type=jnp.float32)
        tok_ref[ALL] = vals.astype(jnp.bfloat16)
        inv_rms = lax.rsqrt(jnp.mean(vals * vals, axis=LAST, keepdims=True) + RMS_EPS)
        normed = (vals * inv_rms * gain_ref[ALL]).astype(jnp.bfloat16)
        norm_ref[ALL] = normed
        own_ref[ALL], give_ref[ALL] = side_blocks(normed, side_s[0], n_dev)

    def row_block(cols):
        return pl.BlockSpec((NORM_ROWS, cols), lambda step, side: (step, 0))

    def whole(rows):
        return pl.BlockSpec((rows, width), lambda step, side: (0, 0))

    shape = lambda cols: jax.ShapeDtypeStruct((tok_count, cols), jnp.bfloat16)
    return pl.pallas_call(
        kernel,
        grid_spec=pltpu.PrefetchScalarGridSpec(
            num_scalar_prefetch=1,
            grid=(tok_count // NORM_ROWS,),
            in_specs=[row_block(128), whole(n_slots), whole(1)],
            out_specs=(row_block(width), row_block(width), row_block(width // 2), row_block(width // 2)),
        ),
        out_shape=(shape(width), shape(width), shape(width // 2), shape(width // 2)),
        compiler_params=pltpu.CompilerParams(vmem_limit_bytes=MUCH_VMEM),
        cost_estimate=cost_of(2 * tok_count * n_slots * width),
        name='expand_rows',
    )(side.reshape(1), slot_cols, slot_rows, gain_f32.reshape(1, width))


def grad_rows_of(left, right, tile=GRAD_TILE):
    tok_count, left_dim = left[0].shape
    n_cols = right[0].shape[COL]
    block = 256

    def kernel(left_own, left_sib, right_own, right_sib, out_ref):
        for at in range(0, left_dim, block):
            vals = lax.dot_general(left_own[:, at:at + block], right_own[ALL], ROW_DIMS, preferred_element_type=jnp.float32)
            out_ref[at:at + block, :] = vals + lax.dot_general(left_sib[:, at:at + block], right_sib[ALL], ROW_DIMS, preferred_element_type=jnp.float32)

    whole = pl.BlockSpec((tok_count, left_dim), lambda step: (0, 0))
    part = pl.BlockSpec((tok_count, tile), lambda step: (0, step))
    return pl.pallas_call(
        kernel,
        grid=(n_cols // tile,),
        in_specs=[whole, whole, part, part],
        out_specs=pl.BlockSpec((left_dim, tile), lambda step: (0, step)),
        out_shape=jax.ShapeDtypeStruct((left_dim, n_cols), jnp.float32),
        compiler_params=pltpu.CompilerParams(vmem_limit_bytes=MUCH_VMEM),
        cost_estimate=cost_of(4 * tok_count * left_dim * n_cols),
        name='grad_rows_of',
    )(*left, *right)


def fold_rows(slot_of, d_normed, slot_dy, slot_rows, gain_f32, n_dev):
    n_slots, width = slot_rows.shape
    tok_count = slot_of.shape[ROW]
    sizes = [BASE_CAP] * n_dev + [HEAVY_CAP - RELAY_ROWS, RELAY_ROWS]

    def kernel(at_ref, dn_ref, dy_ref, rows_ref, gain_ref, *out_refs):
        start = 0
        for out_ref, size in zip(out_refs, sizes):
            place = slice(start, start + size)
            slot = start + row_iota((size, tok_count))
            chooser = (slot == at_ref[ALL]).astype(jnp.float32).astype(jnp.bfloat16)
            d_norm = jnp.dot(chooser, dn_ref[ALL], preferred_element_type=jnp.float32)
            out_ref[ALL] = dy_ref[place] + norm_back(rows_ref[place].astype(jnp.float32), d_norm, gain_ref[ALL])
            start += size

    return pl.pallas_call(
        kernel,
        out_shape=tuple(jax.ShapeDtypeStruct((size, width), jnp.float32) for size in sizes),
        in_specs=[pl.BlockSpec(memory_space=pltpu.VMEM)] * 5,
        out_specs=tuple(pl.BlockSpec(memory_space=pltpu.VMEM) for _ in sizes),
        compiler_params=pltpu.CompilerParams(vmem_limit_bytes=MOST_VMEM),
        cost_estimate=cost_of(2 * tok_count * n_slots * width),
        name='fold_rows',
    )(slot_of.reshape(1, tok_count), d_normed, slot_dy, slot_rows, gain_f32.reshape(1, width))


def hop_send(vals, hop, n_dev):
    return lax.ppermute(vals, 'fsdp', [(dev, dev ^ hop) for dev in range(n_dev)])


def side_scatter(vals, n_dev):
    groups = [list(range(side, n_dev, 2)) for side in range(2)]
    return lax.psum_scatter(vals, 'fsdp', scatter_dimension=0, tiled=True, axis_index_groups=groups)


def solution(mesh):
    tok_spec = P(('dp', 'fsdp'), None)
    seq_spec = P(('dp', 'fsdp'), None, None)
    part_vec = P(('dp', 'fsdp'))
    vec_spec = P('fsdp')
    mat_spec = P('fsdp', None)

    def device_step(tok_ids, grad_out, emb_table, norm_gain, w_query, w_kv_down, kv_gain, w_kv_up, w_out):
        seq_count, seq_len = tok_ids.shape
        vocab_dev, d_model = emb_table.shape
        tok_count = seq_count * seq_len
        kv_rank = w_kv_down.shape[COL] - ROPE_DIM
        n_dev = mesh.shape['fsdp']
        my_dev = lax.axis_index('fsdp')
        side = lax.rem(my_dev, PAIR)
        n_slots = n_dev * BASE_CAP + HEAVY_CAP
        flat_ids = tok_ids.reshape(tok_count)
        grad_rows = grad_out.reshape(tok_count, d_model)

        owner, owner_rank, is_first, counts = plan_ids(flat_ids, vocab_dev, n_dev)

        def token_slots(turn):
            return slots_of(owner, owner_rank, my_dev, n_dev, turn)

        note = [slot_list(flat_ids, token_slots(0), is_first, n_slots), flat_ids, counts, norm_gain, kv_gain]
        note = jnp.concatenate([piece.astype(jnp.float32) for piece in note])
        note = jnp.pad(note, (0, -note.shape[ROW] % 128))
        notes = lax.all_gather(note, 'fsdp')
        ends = [0]
        for size in (n_slots, tok_count, n_dev, norm_gain.shape[ROW], kv_gain.shape[ROW]):
            ends.append(ends[-1] + size)
        all_slots, all_ids, all_counts, all_gains, all_kv_gains = (notes[:, low:high] for low, high in zip(ends[:-1], ends[1:]))
        all_slots, all_ids, all_counts = (piece.astype(jnp.int32) for piece in (all_slots, all_ids, all_counts))
        gain_f32, kv_gain_f32 = all_gains.reshape(-1), all_kv_gains.reshape(-1)
        caps = owner_cap(jnp.arange(n_dev))
        turns = jnp.max((all_counts + caps - 1) // caps)

        w_out_full = lax.all_gather(w_out, 'fsdp', tiled=True)
        query_shard, down_shard = after(tuple(arrange_weights(w_query, w_kv_down)), notes)
        w_query_full = lax.all_gather(query_shard, 'fsdp', tiled=True)
        w_down_full = lax.all_gather(down_shard, 'fsdp', tiled=True)

        def turn_lists(turn):
            def one_dev(ids, dev, turn):
                its_owner, its_rank, its_first, _ = plan_ids(ids, vocab_dev, n_dev)
                return slot_list(ids, slots_of(its_owner, its_rank, dev, n_dev, turn), its_first, n_slots)

            ids, turn = lax.optimization_barrier((all_ids, jnp.asarray(turn, jnp.int32)))
            return wanted_lists(jax.vmap(one_dev, (0, 0, None))(ids, jnp.arange(n_dev), turn), my_dev, n_dev)

        def spread_of(turn):
            return (token_slots(turn)[:, NEW] == jnp.arange(n_slots)[NEW, :]).astype(jnp.bfloat16)

        def fetch_rows(lists):
            return swap_rows(pick_rows(emb_table, lists, my_dev), n_dev)

        def expand(turn, slot_rows):
            return jnp.dot(spread_of(turn), slot_rows, preferred_element_type=jnp.float32).astype(jnp.bfloat16)

        def expand_more(step, have):
            rows = lax.fori_loop(1, turns, lambda turn, have: have + expand(turn, fetch_rows(turn_lists(turn))), expand(0, slot_rows))
            normed = rms_scale(rows, gain_f32)
            return (rows, normed) + side_blocks(normed, side, n_dev)

        lists = wanted_lists(all_slots, my_dev, n_dev)
        first_plan = table_plan(lists, my_dev, vocab_dev)
        work = (token_slots(0).reshape(1, tok_count), grad_rows, w_out_full)
        slot_rows, slot_dy, d_mix = swap_rows(pick_rows(emb_table, lists, my_dev), n_dev, work)
        many = (turns > 1).astype(jnp.int32)
        first_rows = tuple(expand_rows(token_slots(0), slot_rows, gain_f32, side, n_dev))
        tok_rows, normed, x_own, x_give = lax.fori_loop(0, many, expand_more, first_rows)

        w_up_full = lax.all_gather(after(w_kv_up, slot_rows), 'fsdp', tiled=True)
        down = jnp.dot(normed, w_down_full, preferred_element_type=jnp.float32).astype(jnp.bfloat16)
        latent, latent_pull = jax.vjp(rms_scale, down[:, :kv_rank], kv_gain_f32)
        kv_all = jnp.dot(latent, w_up_full, preferred_element_type=jnp.float32).astype(jnp.bfloat16)
        q_all = jnp.dot(normed, w_query_full, preferred_element_type=jnp.float32).astype(jnp.bfloat16)
        x_both = (x_own, hop_send(x_give, 1, n_dev))
        dy_both = (grad_rows, hop_send(grad_rows, 1, n_dev))
        latent_own, latent_give = side_blocks(latent, side, n_dev)
        latent_both = (latent_own, hop_send(latent_give, 1, n_dev))
        mix, mix_own, mix_give, d_query, d_up, d_pe = attend_pairs(q_all, kv_all, down[:, kv_rank:], d_mix, seq_count, side)

        dq_both = (d_query, hop_send(d_query, 1, n_dev))
        mix_both = (mix_own, hop_send(mix_give, 1, n_dev))
        dup_both = (d_up, hop_send(d_up, 1, n_dev))
        d_latent = lax.dot_general(d_up, w_up_full, COL_DIMS, preferred_element_type=jnp.float32).astype(jnp.bfloat16)
        d_w_query = grad_rows_of((after(x_both[0], d_latent), x_both[1]), dq_both)
        g_query = side_scatter(d_w_query, n_dev)
        d_ckv, d_kv_gain = latent_pull(after(d_latent, d_w_query))
        d_down = jnp.concatenate([d_ckv, d_pe], axis=COL)
        d_normed = lax.dot_general(after(d_query, d_w_query), w_query_full, COL_DIMS, preferred_element_type=jnp.float32)
        d_normed = d_normed + lax.dot_general(d_down, w_down_full, COL_DIMS, preferred_element_type=jnp.float32)
        d_normed = d_normed.astype(jnp.bfloat16)
        parts = fold_rows(token_slots(0), d_normed, slot_dy, slot_rows, gain_f32, n_dev)
        pieces = permute_rows(parts, n_dev)

        d_w_out = grad_rows_of((after(mix_both[0], *parts), mix_both[1]), dy_both)
        toks_f32 = after(tok_rows, d_w_out).astype(jnp.float32)
        gains = jnp.concatenate([gain_back(toks_f32, d_normed.astype(jnp.float32)), d_kv_gain])
        gains = gains + hop_send(gains, 1, n_dev)
        down_both = (after(d_down, d_w_out), hop_send(d_down, 1, n_dev))
        d_w_down = grad_rows_of(x_both, down_both, LANES)
        gain_col = lax.dynamic_index_in_dim(gains[:d_model].reshape(-1, 2, d_model // n_dev), side, 1, False)
        kv_gain_col = lax.dynamic_index_in_dim(gains[d_model:].reshape(-1, 2, kv_rank // n_dev), side, 1, False)
        kv_gain_col = jnp.pad(kv_gain_col, ((0, 0), (0, (d_model - kv_rank) // n_dev)))
        col_at = jnp.arange(d_w_down.shape[COL])[NEW, :]
        gain_at, kv_gain_at = kv_rank + HALF_ROPE, kv_rank + ROPE_DIM + HALF_ROPE
        d_w_down = jnp.where(col_at == gain_at, gain_col.reshape(-1, 1), jnp.where(col_at == kv_gain_at, kv_gain_col.reshape(-1, 1), d_w_down))
        d_w_out_down = jnp.concatenate([d_w_out, d_w_down], axis=COL)
        d_w_up = grad_rows_of((after(latent_both[0], d_w_out_down), latent_both[1]), dup_both)
        g_up = side_scatter(d_w_up, n_dev)
        block_out = (toks_f32 + jnp.dot(after(mix, d_w_up), w_out_full, preferred_element_type=jnp.float32)).astype(jnp.bfloat16)
        g_out_down = side_scatter(after(d_w_out_down, pieces, d_w_up, block_out), n_dev)
        g_out, g_down = g_out_down[:, :d_model], g_out_down[:, d_model:]

        def many_turns(step, table):
            d_rows = grad_rows.astype(jnp.float32) + norm_back(tok_rows.astype(jnp.float32), d_normed.astype(jnp.float32), gain_f32)

            def add_turn(turn, table):
                slot_grads = lax.dot_general(spread_of(turn).astype(jnp.float32), d_rows, ROW_DIMS, precision=lax.Precision.HIGHEST, preferred_element_type=jnp.float32)
                return write_table(return_rows(slot_grads, n_dev), table_plan(turn_lists(turn), my_dev, vocab_dev), my_dev, vocab_dev, jnp.float32, table)

            return lax.fori_loop(0, turns, add_turn, jnp.zeros((vocab_dev, d_model), jnp.float32)).astype(jnp.bfloat16)

        g_query = head_columns(g_query)
        grad_table = lax.fori_loop(0, many, many_turns, write_table(pieces, first_plan, my_dev, vocab_dev, jnp.bfloat16))
        g_pe = [g_down[:, kv_rank:kv_rank + HALF_ROPE], g_down[:, kv_rank + ROPE_DIM:kv_rank + ROPE_DIM + HALF_ROPE]]
        grads = (g_down[:, gain_at], g_query, jnp.concatenate([g_down[:, :kv_rank]] + g_pe, axis=COL), g_down[:kv_gain.shape[ROW], kv_gain_at], g_up, g_out)
        return (block_out.reshape(seq_count, seq_len, d_model), grad_table) + grads

    return jax.shard_map(device_step, mesh=mesh, in_specs=(tok_spec, seq_spec, mat_spec, vec_spec, mat_spec, mat_spec, vec_spec, mat_spec, mat_spec), out_specs=(seq_spec, tok_spec, part_vec, tok_spec, tok_spec, part_vec, tok_spec, tok_spec), check_vma=False)
```

time: 2500 us -> 1010 us (0.40)
  local copies, waits for them, and re-layouts: 601 us -> 49.7 us
  other arithmetic: 589 us -> 48 us
  Pallas kernels: 0 us -> 496 us
  matrix products: 449 us -> 109 us
  waiting for transfers between devices: 567 us -> 250 us
  blocking collectives: 255 us -> 11.5 us
    pallas_call x0 -> x11, Pallas kernels: none -> 496 us  [the longest x1 151 us: swap_rows(): pl.pallas_call(kernel, out_shape=tuple(out_shape), in_specs=in_specs, out...]
    gather x1 -> x0, local copies, waits for them, and re-layouts: 444 us -> none  [device_step(): picked = jnp.take(emb_table, jnp.where(is_owned, local_ids, 0), axis=0)]
    scatter-add x3 -> x0, other arithmetic: 380 us -> none  [device_step(): jax.ops.segment_sum(all_grads, seg_ids, num_segments=vocab_dev)]
    all_gather x5 -> x4, waiting for transfers between devices: 348 us -> 0.07 us  [the longest x1 0.02 us: device_step(): w_out_full = lax.all_gather(w_out, 'fsdp', tiled=True)]
    dot_general x21 -> x7, matrix products: 449 us -> 109 us  [the longest x1 25.7 us: device_step(): jnp.dot(normed, w_query_full, preferred_element_type=jnp.float32)]
    unnamed x2 -> x0, blocking collectives: 236 us -> none
    ppermute x0 -> x25, waiting for transfers between devices: none -> 205 us  [the longest x7 114 us: permute_rows(): lax.ppermute(base[hop], 'fsdp', [(dev, dev ^ hop) for dev in range(n_dev)])]
    reduce_scatter x5 -> x3, waiting for transfers between devices: 217 us -> 43.1 us  [side_scatter(): lax.psum_scatter(vals, 'fsdp', scatter_dimension=0, tiled=True, axis_inde...]
  transfers between devices with their start and end apart: 10 -> 32, of which waited for: 3 -> 13; matrix products, arithmetic and copies ran while one was open for 47% -> 18% of each run, Pallas kernels for 0% -> 40%
where the time goes in v1:
time: 1010 us; the launch traced here: 1000 us
  Pallas kernels  496 us (49%)
  waiting for transfers between devices  250 us (25%)
  matrix products  109 us (11%)
  local copies, waits for them, and re-layouts  49.7 us (5%)
  other arithmetic  48 us (5%)
  starting transfers between devices  23.7 us (2%)
  between operations  16.1 us (2%)
  blocking collectives  11.5 us (1%)
    pallas_call x1, Pallas kernels, swap_rows(): pl.pallas_call(kernel, out_shape=tuple(out_shape), in_specs=in_specs, out...  151 us
    ppermute x7, waiting for transfers between devices, permute_rows(): lax.ppermute(base[hop], 'fsdp', [(dev, dev ^ hop) for dev in range(n_dev)])  114 us
    pallas_call x1, Pallas kernels, write_table(): pl.pallas_call(kernel, out_shape=jax.ShapeDtypeStruct((vocab_dev, width),...  89.5 us
    pallas_call x1, Pallas kernels, pick_rows(): pl.pallas_call(kernel, out_shape=jax.ShapeDtypeStruct((n_dev * DEST_ROWS,...  70 us
    pallas_call x4, Pallas kernels, grad_rows_of(): pl.pallas_call(kernel, grid=(n_cols // tile,), in_specs=[whole, whole, pa...  69.7 us
    pallas_call x1, Pallas kernels, attend_pairs(): pl.pallas_call(kernel, grid_spec=pltpu.PrefetchScalarGridSpec(num_scalar_...  67.8 us
    reduce_scatter x3, waiting for transfers between devices, side_scatter(): lax.psum_scatter(vals, 'fsdp', scatter_dimension=0, tiled=True, axis_inde...  43.1 us
    ppermute x2, waiting for transfers between devices, permute_rows(): arrived[source].append(lax.ppermute(passed, 'fsdp', [(source - 4, 0)]))  39.3 us
  transfers between devices with their start and end apart: 32, of which 13 were waited for; matrix products, arithmetic and copies ran while one was open for 18% of the time, Pallas kernels for 40%

profile of v1, /device:TPU:0, one launch (start us, length us, event | category | flops | bytes accessed | tf_op | source)
XLA Modules:
  0.0 1004.9 jit_solution(16947614691072945497)
XLA Ops:
  16.8 11.5 %all-gather.1 = f32[8,1,3584]{2,1,0:T(1,128)S(1)} all-gather(f32[1,1,3584]{2,1,0:T(1,128)S(1)} %reshape.727), channel_id=2, replica_groups=mesh['dp'=2,'fsdp'=8] {'fsdp'}, dimensions={0}, use_global_device_ids=true | all-gather | bytes 129024 | tf_op jit(solution)/shard_map/all_gather | solution.py:927
  45.4 70.0 %pick_rows.2.refs_0_ = bf16[4992,2048]{1,0:T(8,128)(2,1)} custom-call(s32[4992]{0:T(1024)} %get-tuple-element.1229.tiles_s, s32[1]{0:T(128)} %bitcast.3.dev_s, bf16[12800,2048]{1,0:T(8,128)(2,1)} %table_ref.1, s32[4992,128]{1,0:T(8,128)} %broadcast_in_dim.534.tags_ref), custom_call_target="tpu_custom_call" | custom-call | flops 4000000000 | bytes 100000000 | tf_op jit(solution)/shard_map/pick_rows/pallas_call | solution.py:353
  115.5 151.1 %swap_rows.5 = (bf16[1632,2048]{1,0:T(8,128)(2,1)}, bf16[240,2048]{1,0:T(8,128)(2,1)}, f32[1632,2048]{1,0:T(8,128)}, bf16[1536,2048]{1,0:T(8,128)(2,1)}) custom-call(bf16[4992,2048]{1,0:T(8,128)(2,1)} %pick_rows.2.refs_0_, s32[1,1536]{1,0:T(1,128)S(1)} %and_select_fusion.refs_1_.at_ref, bf16[1536,2048]{1,0:T(8,128)(2,1)} %bitcast.77, ...), custom_call_target="tpu_custom_call" | custom-call | flops 20000000000 | bytes 100000000 | tf_op jit(solution)/shard_map/swap_rows/pallas_call | solution.py:527
  266.9 19.2 %expand_rows.1 = (bf16[1536,2048]{1,0:T(8,128)(2,1)}, bf16[1536,2048]{1,0:T(8,128)(2,1)}, bf16[1536,1024]{1,0:T(8,128)(2,1)}, bf16[1536,1024]{1,0:T(8,128)(2,1)}) custom-call(s32[1]{0:T(128)} %bitcast.2.side_s, s32[1536,128]{1,0:T(8,128)S(1)} %broadcast_in_dim.525.at_ref, bf16[1632,2048]{1,0:T(8,128)(2,1)} %get-tuple-element.1764.rows_ref, ...), custom_call_target="tpu_custom_call" | custom-call | flops 10267656192 | bytes 100000000 | tf_op jit(solution)/shard_map/expand_rows/pallas_call | solution.py:826
  296.6 25.7 %convolution_convert_fusion.1.q_ref = bf16[1536,3072]{1,0:T(8,128)(2,1)} fusion(bf16[1536,2048]{1,0:T(8,128)(2,1)} %get-tuple-element.994, bf16[2048,3072]{1,0:T(8,128)(2,1)} %all-gather.9.cloned.1.call-done), kind=kOutput, calls=%fused_computation.141 | convolution fusion | flops 19332071424 | bytes 28311552 | tf_op jit(solution)/shard_map/dot_general | solution.py:976
  322.4 11.8 %convolution_convert_fusion.kv_ref = bf16[1536,4096]{1,0:T(8,128)(2,1)} fusion(bf16[1536,512]{1,0:T(8,128)(2,1)S(1)} %fusion.46, bf16[512,4096]{1,0:T(8,128)(2,1)} %all-gather.13.cloned.1.call-done), kind=kOutput, calls=%fused_computation.134 | convolution fusion | flops 6448742400 | bytes 18350080 | tf_op jit(solution)/shard_map/dot_general | solution.py:975
  334.1 67.8 %attend_pairs.1 = (bf16[1536,2048]{1,0:T(8,128)(2,1)}, bf16[1536,1024]{1,0:T(8,128)(2,1)S(1)}, bf16[1536,1024]{1,0:T(8,128)(2,1)}, bf16[1536,3072]{1,0:T(8,128)(...) custom-call(s32[1]{0:T(128)} %bitcast.2.side_s, bf16[1536,3072]{1,0:T(8,128)(2,1)} %convolution_convert_fusion.1.q_ref, ...), custom_call_target="tpu_custom_call" | custom-call | flops 20000000000 | bytes 100000000 | tf_op jit(solution)/shard_map/attend_pairs/pallas_call | solution.py:219
  402.5 11.3 %convolution_convert_fusion.3 = bf16[1536,512]{1,0:T(8,128)(2,1)} fusion(bf16[1536,4096]{1,0:T(8,128)(2,1)} %get-tuple-element.1004.right_own, bf16[512,4096]{1,0:T(8,128)(2,1)S(1)} %copy-done.60), kind=kOutput, calls=%fused_computation.166 | convolution fusion | flops 6443237376 | bytes 18350080 | tf_op jit(solution)/shard_map/dot_general | solution.py:986
  421.4 24.0 %grad_rows_of.4 = f32[1024,3072]{1,0:T(8,128)} custom-call(bf16[1536,1024]{1,0:T(8,128)(2,1)S(1)} %copy-done.66, bf16[1536,1024]{1,0:T(8,128)(2,1)S(1)} %collective-permute-done.left_sib, bf16[1536,3072]{1,0:T(8,128)(2,1)} %get-tuple-element.1007.right_own, bf16[1536,3072]{1,0:T(8,128)(2,1)} %collective-permute-done.1.right_sib), custom_call_target="tpu_custom_call" | custom-call | flops 19327352832 | bytes 100000000 | tf_op jit(solution)/shard_map/grad_rows_of/pallas_call | solution.py:853
  462.5 24.6 %add_convert_fusion.dn_ref = bf16[1536,2048]{1,0:T(8,128)(2,1)} fusion(f32[1536,2048]{1,0:T(8,128)} %fusion.98, bf16[1536,3072]{1,0:T(8,128)(2,1)} %get-tuple-element.1007.right_own, bf16[2048,3072]{1,0:T(8,128)(2,1)S(1)} %bitcast.104), kind=kOutput, calls=%fused_computation.140 | convolution fusion | flops 19333644288 | bytes 40894464 | tf_op jit(solution)/shard_map/dot_general | solution.py:991
  487.1 25.2 %fold_rows.1 = (f32[144,2048]{1,0:T(8,128)}, f32[144,2048]{1,0:T(8,128)}, f32[144,2048]{1,0:T(8,128)}, f32[144,2048]{1,0:T(8,128)}, f32[144,2048]{1,0:T(8,128)},...) custom-call(s32[1,1536]{1,0:T(1,128)} %copy-done.4, ...), custom_call_target="tpu_custom_call" | custom-call | flops 10267656192 | bytes 100000000 | tf_op jit(solution)/shard_map/fold_rows/pallas_call | solution.py:880
  516.5 18.0 %grad_rows_of.5 = f32[1024,2048]{1,0:T(8,128)} custom-call(bf16[1536,1024]{1,0:T(8,128)(2,1)S(1)} %copy-done.9, bf16[1536,1024]{1,0:T(8,128)(2,1)} %collective-permute-done.2.left_sib, bf16[1536,2048]{1,0:T(8,128)(2,1)} %bitcast.79, bf16[1536,2048]{1,0:T(8,128)(2,1)} %collective-permute-done.3.right_sib), custom_call_target="tpu_custom_call" | custom-call | flops 12884901888 | bytes 100000000 | tf_op jit(solution)/shard_map/grad_rows_of/pallas_call | solution.py:853
  539.2 9.9 fusion.38
  562.0 43.9 %collective-permute-done.12.refs_6_ = f32[144,2048]{1,0:T(8,128)S(1)} collective-permute-done((f32[144,2048]{1,0:T(8,128)}, f32[144,2048]{1,0:T(8,128)S(1)}, u32[]{:S(2)}, u32[]{:S(2)}) %collective-permute-start.12) | collective-permute-done | bytes 1179680 | tf_op jit(solution)/shard_map/ppermute | solution.py:557
  607.8 36.4 %collective-permute-done.16.refs_10_ = f32[144,2048]{1,0:T(8,128)S(1)} collective-permute-done((f32[144,2048]{1,0:T(8,128)S(1)}, f32[144,2048]{1,0:T(8,128)S(1)}, u32[]{:S(2)}, u32[]{:S(2)}) %collective-permute-start.16) | collective-permute-done | bytes 1179680 | tf_op jit(solution)/shard_map/ppermute | solution.py:557
  646.5 26.5 %collective-permute-done.22.refs_15_ = f32[144,2048]{1,0:T(8,128)S(1)} collective-permute-done((f32[144,2048]{1,0:T(8,128)S(1)}, f32[144,2048]{1,0:T(8,128)S(1)}, u32[]{:S(2)}, u32[]{:S(2)}) %collective-permute-start.22) | collective-permute-done | bytes 1179680 | tf_op jit(solution)/shard_map/ppermute | solution.py:557
  690.4 14.3 %grad_rows_of.6 = f32[1024,640]{1,0:T(8,128)} custom-call(bf16[1536,1024]{1,0:T(8,128)(2,1)} %get-tuple-element.1005.left_own, bf16[1536,1024]{1,0:T(8,128)(2,1)} %copy-done.5, bf16[1536,640]{1,0:T(8,128)(2,1)S(1)} %pad_maximum_fusion.4.right_own, bf16[1536,640]{1,0:T(8,128)(2,1)S(1)} %copy-done.7), custom_call_target="tpu_custom_call" | custom-call | flops 4026531840 | bytes 100000000 | tf_op jit(solution)/shard_map/grad_rows_of/pallas_call | solution.py:853
  718.3 35.4 %collective-permute-done.24.refs_17_ = f32[240,2048]{1,0:T(8,128)} collective-permute-done((f32[240,2048]{1,0:T(8,128)}, f32[240,2048]{1,0:T(8,128)}, u32[]{:S(2)}, u32[]{:S(2)}) %collective-permute-start.24) | collective-permute-done | bytes 1966112 | tf_op jit(solution)/shard_map/ppermute | solution.py:556
  760.2 9.2 pad_maximum_fusion.2
  769.4 13.3 %grad_rows_of.7 = f32[256,4096]{1,0:T(8,128)S(1)} custom-call(bf16[1536,256]{1,0:T(8,128)(2,1)S(1)} %get-tuple-element.1026.left_own, bf16[1536,256]{1,0:T(8,128)(2,1)S(1)} %collective-permute-done.6.left_sib, bf16[1536,4096]{1,0:T(8,128)(2,1)} %get-tuple-element.1004.right_own, bf16[1536,4096]{1,0:T(8,128)(2,1)} %collective-permute-done.7.right_sib), custom_call_target="tpu_custom_call" | custom-call | flops 6442450944 | bytes 100000000 | tf_op jit(solution)/shard_map/grad_rows_of/pallas_call | solution.py:853
  784.7 20.1 %fusion.40 = bf16[1536,2048]{1,0:T(8,128)(2,1)} fusion(bf16[1536,2048]{1,0:T(8,128)(2,1)} %get-tuple-element.1023, bf16[1536,2048]{1,0:T(8,128)(2,1)} %get-tuple-element.1027, bf16[2048,2048]{1,0:T(8,128)(2,1)} %all-gather.7.cloned.1.call-done.refs_3_), kind=kOutput, calls=%fused_computation.139 | convolution fusion | flops 12894339072 | bytes 27262976 | tf_op jit(solution)/shard_map/dot_general | solution.py:1012
  804.8 35.0 %collective-permute-done.13.refs_7_ = f32[480,2048]{1,0:T(8,128)} collective-permute-done((f32[480,2048]{1,0:T(8,128)}, f32[480,2048]{1,0:T(8,128)}, u32[]{:S(2)}, u32[]{:S(2)}) %collective-permute-start.13) | collective-permute-done | bytes 3932192 | tf_op jit(solution)/shard_map/ppermute | solution.py:554
  849.0 89.5 %write_table.5 = bf16[12800,2048]{1,0:T(8,128)(2,1)} custom-call(s32[800]{0:T(1024)} %reshape.719.firsts_s, s32[800]{0:T(1024)} %reshape.720.counts_s, s32[1]{0:T(128)} %bitcast.3.dev_s, f32[144,2048]{1,0:T(8,128)} %get-tuple-element.1011.refs_0_, f32[480,2048]{1,0:T(8,128)} %constant_dynamic-update-slice_fusion.refs_1_, f32[144,2048]{1,0:T(8,128)} %copy-done.27, ...), custom_call_target="tpu_custom_call" | custom-call | flops 4000000000 | bytes 100000000 | tf_op jit(solution)/shard_map/write_table/pallas_call | solution.py:764
  954.6 43.1 %reduce-scatter.8.cloned.1.call-done = f32[64,4096]{1,0:T(8,128)} async-done(((f32[256,4096]{1,0:T(8,128)}), f32[64,4096]{1,0:T(8,128)}) %reduce-scatter.8.cloned.1.call-update) | async-done | bytes 1048592 | tf_op jit(solution)/shard_map/reduce_scatter | solution.py:897
  (283 shorter events, 151.8 us)
Async XLA Ops:
  7.2 108.3 %all-gather.7.cloned.1.call-start = ((), (), s32[]{:S(2)}) async-start(), calls=%async_computation.3 | async-start | bytes 9437184 | tf_op jit(solution)/shard_map/all_gather | solution.py:937
  7.9 278.5 %all-gather.11.cloned.1.call-start = ((), (), s32[]{:S(2)}) async-start(), calls=%async_computation.5 | async-start | bytes 2949120 | tf_op jit(solution)/shard_map/all_gather | solution.py:940
  35.6 261.0 %all-gather.9.cloned.1.call-start = ((), (), s32[]{:S(2)}) async-start(), calls=%async_computation.4 | async-start | bytes 14155776 | tf_op jit(solution)/shard_map/all_gather | solution.py:939
  36.3 286.0 %all-gather.13.cloned.1.call-start = ((), (), s32[]{:S(2)}) async-start(), calls=%async_computation.6 | async-start | bytes 4718592 | tf_op jit(solution)/shard_map/all_gather | solution.py:972
  266.6 672.2 %reduce-scatter.6.cloned.1.call-start = ((), (), s32[]{:S(2)}) async-start(), calls=%async_computation.8 | async-start | bytes 15728640 | tf_op jit(solution)/shard_map/reduce_scatter | solution.py:897
  447.1 501.1 %reduce-scatter.4.cloned.1.call-start = ((), (), s32[]{:S(2)}) async-start(), calls=%async_computation.7 | async-start | bytes 13762560 | tf_op jit(solution)/shard_map/reduce_scatter | solution.py:897
  447.5 65.4 %collective-permute-start.3 = (bf16[1536,2048]{1,0:T(8,128)(2,1)}, bf16[1536,2048]{1,0:T(8,128)(2,1)}, u32[]{:S(2)}, u32[]{:S(2)}) collective-permute-start(bf16[1536,2048]{1,0:T(8,128)(2,1)} %bitcast.78), channel_id=1, source_target_pairs={{0,1},{1,0},{2,3},{3,2},{4,5},{5,4},{6,7},{7,6},{8,9},{9,8},{10,11... | collective-permute-start | bytes 18874376 | tf_op jit(solution)/shard_map/ppermute | solution.py:892
  449.6 99.5 %collective-permute-start.6 = (bf16[1536,256]{1,0:T(8,128)(2,1)S(1)}, bf16[1536,256]{1,0:T(8,128)(2,1)S(1)}, u32[]{:S(2)}, u32[]{:S(2)}) collective-permute-start(bf16[1536,256]{1,0:T(8,128)(2,1)S(1)} %get-tuple-element.1213), channel_id=1, source_target_pairs={{0,1},{1,0},{2,3},{3,2},{4,5},{5,4},{6,7},{7,6},{8,9},{9,8},{10,11... | collective-permute-start | bytes 2359304 | tf_op jit(solution)/shard_map/ppermute | solution.py:892
  450.0 267.0 %collective-permute-start.7 = (bf16[1536,4096]{1,0:T(8,128)(2,1)}, bf16[1536,4096]{1,0:T(8,128)(2,1)}, u32[]{:S(2)}, u32[]{:S(2)}) collective-permute-start(bf16[1536,4096]{1,0:T(8,128)(2,1)} %get-tuple-element.1004.right_own), channel_id=1, source_target_pairs={{0,1},{1,0},{2,3},{3,2},{4,5},{5,4},{6,7},{7,6},{8,9},{9,8},{10,11... | collective-permute-start | bytes 37748744 | tf_op jit(solution)/shard_map/ppermute | solution.py:892
  450.2 64.3 %collective-permute-start.2 = (bf16[1536,1024]{1,0:T(8,128)(2,1)}, bf16[1536,1024]{1,0:T(8,128)(2,1)}, u32[]{:S(2)}, u32[]{:S(2)}) collective-permute-start(bf16[1536,1024]{1,0:T(8,128)(2,1)} %get-tuple-element.1022), channel_id=1, source_target_pairs={{0,1},{1,0},{2,3},{3,2},{4,5},{5,4},{6,7},{7,6},{8,9},{9,8},{10,11... | collective-permute-start | bytes 9437192 | tf_op jit(solution)/shard_map/ppermute | solution.py:892
  514.5 91.4 %collective-permute-start.12 = (f32[144,2048]{1,0:T(8,128)}, f32[144,2048]{1,0:T(8,128)S(1)}, u32[]{:S(2)}, u32[]{:S(2)}) collective-permute-start(f32[144,2048]{1,0:T(8,128)} %get-tuple-element.1014), channel_id=1, source_target_pairs={{0,3},{1,2},{2,1},{3,0},{4,7},{5,6},{6,5},{7,4},{8,11},{9,10},{10,... | collective-permute-start | bytes 3538952 | tf_op jit(solution)/shard_map/ppermute | solution.py:557
  550.4 55.9 %collective-permute-start.14 = (f32[144,2048]{1,0:T(8,128)S(1)}, f32[144,2048]{1,0:T(8,128)S(1)}, u32[]{:S(2)}, u32[]{:S(2)}) collective-permute-start(f32[144,2048]{1,0:T(8,128)S(1)} %copy-done.65), channel_id=1, source_target_pairs={{0,4},{1,5},{2,6},{3,7},{4,0},{5,1},{6,2},{7,3},{8,12},{9,13},{10,... | collective-permute-start | bytes 3538952 | tf_op jit(solution)/shard_map/ppermute | solution.py:557
  552.5 91.7 %collective-permute-start.16 = (f32[144,2048]{1,0:T(8,128)S(1)}, f32[144,2048]{1,0:T(8,128)S(1)}, u32[]{:S(2)}, u32[]{:S(2)}) collective-permute-start(f32[144,2048]{1,0:T(8,128)S(1)} %copy-done.64), channel_id=1, source_target_pairs={{0,5},{1,4},{2,7},{3,6},{4,1},{5,0},{6,3},{7,2},{8,13},{9,12},{10,... | collective-permute-start | bytes 3538952 | tf_op jit(solution)/shard_map/ppermute | solution.py:557
  560.0 114.3 %collective-permute-start.20 = (f32[240,2048]{1,0:T(8,128)S(1)}, f32[240,2048]{1,0:T(8,128)}, u32[]{:S(2)}, u32[]{:S(2)}) collective-permute-start(f32[240,2048]{1,0:T(8,128)S(1)} %copy-done.25), channel_id=1, source_target_pairs={{6,2},{7,3},{14,10},{15,11}} | collective-permute-start | bytes 5898248 | tf_op jit(solution)/shard_map/ppermute | solution.py:549
  605.9 69.8 %collective-permute-start.5 = (bf16[1536,640]{1,0:T(8,128)(2,1)S(1)}, bf16[1536,640]{1,0:T(8,128)(2,1)S(1)}, u32[]{:S(2)}, u32[]{:S(2)}) collective-permute-start(bf16[1536,640]{1,0:T(8,128)(2,1)S(1)} %pad_maximum_fusion.4.right_own), channel_id=1, source_target_pairs={{0,1},{1,0},{2,3},{3,2},{4,5},{5,4},{6,7},{7,6},{8,9},{9,8},{10,11... | collective-permute-start | bytes 5898248 | tf_op jit(solution)/shard_map/ppermute | solution.py:892
  645.2 64.1 %collective-permute-start.23 = (f32[240,2048]{1,0:T(8,128)}, f32[240,2048]{1,0:T(8,128)}, u32[]{:S(2)}, u32[]{:S(2)}) collective-permute-start(f32[240,2048]{1,0:T(8,128)} %get-tuple-element.1019), channel_id=1, source_target_pairs={{7,0},{15,8}} | collective-permute-start | bytes 5898248 | tf_op jit(solution)/shard_map/ppermute | solution.py:552
  674.4 79.3 %collective-permute-start.24 = (f32[240,2048]{1,0:T(8,128)}, f32[240,2048]{1,0:T(8,128)}, u32[]{:S(2)}, u32[]{:S(2)}) collective-permute-start(f32[240,2048]{1,0:T(8,128)} %collective-permute-done.20), channel_id=1, source_target_pairs={{3,0},{11,8}} | collective-permute-start | bytes 5898248 | tf_op jit(solution)/shard_map/ppermute | solution.py:556
  677.0 81.9 %collective-permute-start.21 = (f32[240,2048]{1,0:T(8,128)}, f32[240,2048]{1,0:T(8,128)}, u32[]{:S(2)}, u32[]{:S(2)}) collective-permute-start(f32[240,2048]{1,0:T(8,128)} %collective-permute-done.20), channel_id=1, source_target_pairs={{2,0},{10,8}} | collective-permute-start | bytes 5898248 | tf_op jit(solution)/shard_map/ppermute | solution.py:556
  709.4 95.4 %collective-permute-start.17 = (f32[480,2048]{1,0:T(8,128)}, f32[480,2048]{1,0:T(8,128)}, u32[]{:S(2)}, u32[]{:S(2)}) collective-permute-start(f32[480,2048]{1,0:T(8,128)} %constant_dynamic-update-slice_fusion.refs_1_), channel_id=1, source_target_pairs={{5,0},{13,8}} | collective-permute-start | bytes 11796488 | tf_op jit(solution)/shard_map/ppermute | solution.py:554
  715.7 89.0 %collective-permute-start.15 = (f32[480,2048]{1,0:T(8,128)}, f32[480,2048]{1,0:T(8,128)}, u32[]{:S(2)}, u32[]{:S(2)}) collective-permute-start(f32[480,2048]{1,0:T(8,128)} %constant_dynamic-update-slice_fusion.refs_1_), channel_id=1, source_target_pairs={{4,0},{12,8}} | collective-permute-start | bytes 11796488 | tf_op jit(solution)/shard_map/ppermute | solution.py:554
  717.0 122.8 %collective-permute-start.13 = (f32[480,2048]{1,0:T(8,128)}, f32[480,2048]{1,0:T(8,128)}, u32[]{:S(2)}, u32[]{:S(2)}) collective-permute-start(f32[480,2048]{1,0:T(8,128)} %constant_dynamic-update-slice_fusion.refs_1_), channel_id=1, source_target_pairs={{3,0},{11,8}} | collective-permute-start | bytes 11796488 | tf_op jit(solution)/shard_map/ppermute | solution.py:554
  753.7 88.3 %collective-permute-start.11 = (f32[480,2048]{1,0:T(8,128)}, f32[480,2048]{1,0:T(8,128)}, u32[]{:S(2)}, u32[]{:S(2)}) collective-permute-start(f32[480,2048]{1,0:T(8,128)} %constant_dynamic-update-slice_fusion.refs_1_), channel_id=1, source_target_pairs={{2,0},{10,8}} | collective-permute-start | bytes 11796488 | tf_op jit(solution)/shard_map/ppermute | solution.py:554
  758.9 83.1 %collective-permute-start.9 = (f32[480,2048]{1,0:T(8,128)}, f32[480,2048]{1,0:T(8,128)}, u32[]{:S(2)}, u32[]{:S(2)}) collective-permute-start(f32[480,2048]{1,0:T(8,128)} %constant_dynamic-update-slice_fusion.refs_1_), channel_id=1, source_target_pairs={{1,0},{9,8}} | collective-permute-start | bytes 11796488 | tf_op jit(solution)/shard_map/ppermute | solution.py:554
  842.1 155.6 %reduce-scatter.8.cloned.1.call-start = ((), (), s32[]{:S(2)}) async-start(), calls=%async_computation.9 | async-start | bytes 5242880 | tf_op jit(solution)/shard_map/reduce_scatter | solution.py:897
  (65 other events, 1937.8 us)
Sparse Core Ops, SparseCore 0:
  9.8 53.7 all-gather.6
  66.0 26.2 all-gather.10
  94.1 118.0 all-gather.8
  266.7 33.4 all-gather.12
  447.2 156.8 reduce-scatter.5
  842.2 103.0 reduce-scatter.3
  948.8 48.8 reduce-scatter.7

commit v2 on v1

--- a/solution.py
+++ b/solution.py
@@ -87,13 +87,15 @@
     )(w_query, w_down, pair_pick, twice_pick)
 
 
-def head_columns(d_query_w):
-    rows = d_query_w.shape[ROW]
-    pairs = d_query_w.reshape(rows, -1, PAIR_DIM)
-    plain = pairs[ALL, :2 * NOPE_DIM].reshape(rows, -1, 2, NOPE_DIM)
-    rotary = pairs[ALL, 2 * NOPE_DIM:].reshape(rows, -1, 2, 2, HALF_ROPE)
-    rotary = jnp.swapaxes(rotary, 2, 3).reshape(rows, -1, 2, ROPE_DIM)
-    return jnp.concatenate([plain, rotary], axis=LAST).reshape(rows, -1)
+def heads_pick():
+    return (jnp.arange(PAIR_DIM)[NEW, :] == pair_source(PAIR_DIM)[:, NEW]).astype(jnp.bfloat16)
+
+
+def split_three(vals):
+    high = vals.astype(jnp.bfloat16)
+    left = vals - high.astype(jnp.float32)
+    mid = left.astype(jnp.bfloat16)
+    return high, mid, (left - mid.astype(jnp.float32)).astype(jnp.bfloat16)
 
 
 def rope_tables(seq_len):
@@ -709,11 +711,7 @@
                 chooser = jnp.concatenate([chooser] * 3, axis=ROW).T.astype(jnp.bfloat16)
                 for col in range(0, width, 512):
                     part = jnp.where(live[:, :1], staged[slot, place, col:col + 512], 0.0)
-                    high = part.astype(jnp.bfloat16)
-                    left = part - high.astype(jnp.float32)
-                    mid = left.astype(jnp.bfloat16)
-                    low = (left - mid.astype(jnp.float32)).astype(jnp.bfloat16)
-                    stacked = jnp.concatenate([high, mid, low], axis=ROW)
+                    stacked = jnp.concatenate(split_three(part), axis=ROW)
                     store(col, jnp.dot(chooser, stacked, preferred_element_type=jnp.float32))
 
             def store_out(col, vals):
@@ -838,28 +836,37 @@
     )(side.reshape(1), slot_cols, slot_rows, gain_f32.reshape(1, width))
 
 
-def grad_rows_of(left, right, tile=GRAD_TILE):
+def grad_rows_of(left, right, tile=GRAD_TILE, pick=None):
     tok_count, left_dim = left[0].shape
     n_cols = right[0].shape[COL]
     block = 256
 
-    def kernel(left_own, left_sib, right_own, right_sib, out_ref):
+    def columns(right_ref, pick_refs):
+        if not pick_refs:
+            return right_ref[ALL]
+        cuts = [right_ref[:, at:at + PAIR_DIM] for at in range(0, tile, PAIR_DIM)]
+        return jnp.concatenate([jnp.dot(cut, pick_refs[0][ALL], preferred_element_type=jnp.float32).astype(jnp.bfloat16) for cut in cuts], axis=COL)
+
+    def kernel(left_own, left_sib, right_own, right_sib, *rest):
+        out_ref = rest[-1]
+        own_cols, sib_cols = columns(right_own, rest[:-1]), columns(right_sib, rest[:-1])
         for at in range(0, left_dim, block):
-            vals = lax.dot_general(left_own[:, at:at + block], right_own[ALL], ROW_DIMS, preferred_element_type=jnp.float32)
-            out_ref[at:at + block, :] = vals + lax.dot_general(left_sib[:, at:at + block], right_sib[ALL], ROW_DIMS, preferred_element_type=jnp.float32)
+            vals = lax.dot_general(left_own[:, at:at + block], own_cols, ROW_DIMS, preferred_element_type=jnp.float32)
+            out_ref[at:at + block, :] = vals + lax.dot_general(left_sib[:, at:at + block], sib_cols, ROW_DIMS, preferred_element_type=jnp.float32)
 
     whole = pl.BlockSpec((tok_count, left_dim), lambda step: (0, 0))
     part = pl.BlockSpec((tok_count, tile), lambda step: (0, step))
+    extras = () if pick is None else (pick,)
     return pl.pallas_call(
         kernel,
         grid=(n_cols // tile,),
-        in_specs=[whole, whole, part, part],
+        in_specs=[whole, whole, part, part] + [pl.BlockSpec(extra.shape, lambda step: (0, 0)) for extra in extras],
         out_specs=pl.BlockSpec((left_dim, tile), lambda step: (0, step)),
         out_shape=jax.ShapeDtypeStruct((left_dim, n_cols), jnp.float32),
         compiler_params=pltpu.CompilerParams(vmem_limit_bytes=MUCH_VMEM),
         cost_estimate=cost_of(4 * tok_count * left_dim * n_cols),
         name='grad_rows_of',
-    )(*left, *right)
+    )(*left, *right, *extras)
 
 
 def fold_rows(slot_of, d_normed, slot_dy, slot_rows, gain_f32, n_dev):
@@ -962,7 +969,6 @@
             return (rows, normed) + side_blocks(normed, side, n_dev)
 
         lists = wanted_lists(all_slots, my_dev, n_dev)
-        first_plan = table_plan(lists, my_dev, vocab_dev)
         work = (token_slots(0).reshape(1, tok_count), grad_rows, w_out_full)
         slot_rows, slot_dy, d_mix = swap_rows(pick_rows(emb_table, lists, my_dev), n_dev, work)
         many = (turns > 1).astype(jnp.int32)
@@ -980,25 +986,26 @@
         latent_both = (latent_own, hop_send(latent_give, 1, n_dev))
         mix, mix_own, mix_give, d_query, d_up, d_pe = attend_pairs(q_all, kv_all, down[:, kv_rank:], d_mix, seq_count, side)
 
+        mix_both = (mix_own, hop_send(mix_give, 1, n_dev))
         dq_both = (d_query, hop_send(d_query, 1, n_dev))
-        mix_both = (mix_own, hop_send(mix_give, 1, n_dev))
         dup_both = (d_up, hop_send(d_up, 1, n_dev))
         d_latent = lax.dot_general(d_up, w_up_full, COL_DIMS, preferred_element_type=jnp.float32).astype(jnp.bfloat16)
-        d_w_query = grad_rows_of((after(x_both[0], d_latent), x_both[1]), dq_both)
-        g_query = side_scatter(d_w_query, n_dev)
-        d_ckv, d_kv_gain = latent_pull(after(d_latent, d_w_query))
+        d_w_out = grad_rows_of((after(mix_both[0], d_latent), mix_both[1]), dy_both)
+        g_out = side_scatter(d_w_out, n_dev)
+        d_ckv, d_kv_gain = latent_pull(after(d_latent, d_w_out))
         d_down = jnp.concatenate([d_ckv, d_pe], axis=COL)
-        d_normed = lax.dot_general(after(d_query, d_w_query), w_query_full, COL_DIMS, preferred_element_type=jnp.float32)
+        d_normed = lax.dot_general(after(d_query, d_w_out), w_query_full, COL_DIMS, preferred_element_type=jnp.float32)
         d_normed = d_normed + lax.dot_general(d_down, w_down_full, COL_DIMS, preferred_element_type=jnp.float32)
         d_normed = d_normed.astype(jnp.bfloat16)
         parts = fold_rows(token_slots(0), d_normed, slot_dy, slot_rows, gain_f32, n_dev)
         pieces = permute_rows(parts, n_dev)
 
-        d_w_out = grad_rows_of((after(mix_both[0], *parts), mix_both[1]), dy_both)
-        toks_f32 = after(tok_rows, d_w_out).astype(jnp.float32)
+        d_w_up = grad_rows_of((after(latent_both[0], *parts), latent_both[1]), dup_both)
+        g_up = side_scatter(d_w_up, n_dev)
+        toks_f32 = after(tok_rows, d_w_up).astype(jnp.float32)
         gains = jnp.concatenate([gain_back(toks_f32, d_normed.astype(jnp.float32)), d_kv_gain])
         gains = gains + hop_send(gains, 1, n_dev)
-        down_both = (after(d_down, d_w_out), hop_send(d_down, 1, n_dev))
+        down_both = (after(d_down, d_w_up), hop_send(d_down, 1, n_dev))
         d_w_down = grad_rows_of(x_both, down_both, LANES)
         gain_col = lax.dynamic_index_in_dim(gains[:d_model].reshape(-1, 2, d_model // n_dev), side, 1, False)
         kv_gain_col = lax.dynamic_index_in_dim(gains[d_model:].reshape(-1, 2, kv_rank // n_dev), side, 1, False)
@@ -1006,12 +1013,11 @@
         col_at = jnp.arange(d_w_down.shape[COL])[NEW, :]
         gain_at, kv_gain_at = kv_rank + HALF_ROPE, kv_rank + ROPE_DIM + HALF_ROPE
         d_w_down = jnp.where(col_at == gain_at, gain_col.reshape(-1, 1), jnp.where(col_at == kv_gain_at, kv_gain_col.reshape(-1, 1), d_w_down))
-        d_w_out_down = jnp.concatenate([d_w_out, d_w_down], axis=COL)
-        d_w_up = grad_rows_of((after(latent_both[0], d_w_out_down), latent_both[1]), dup_both)
-        g_up = side_scatter(d_w_up, n_dev)
-        block_out = (toks_f32 + jnp.dot(after(mix, d_w_up), w_out_full, preferred_element_type=jnp.float32)).astype(jnp.bfloat16)
-        g_out_down = side_scatter(after(d_w_out_down, pieces, d_w_up, block_out), n_dev)
-        g_out, g_down = g_out_down[:, :d_model], g_out_down[:, d_model:]
+        g_down = side_scatter(d_w_down, n_dev)
+        d_w_query = grad_rows_of((after(x_both[0], d_w_down), x_both[1]), dq_both, 2 * PAIR_DIM, heads_pick())
+        block_out = (toks_f32 + jnp.dot(after(mix, d_w_query), w_out_full, preferred_element_type=jnp.float32)).astype(jnp.bfloat16)
+        first_plan = table_plan(after(lists, d_w_query), my_dev, vocab_dev)
+        g_query = side_scatter(after(d_w_query, pieces, block_out), n_dev)
 
         def many_turns(step, table):
             d_rows = grad_rows.astype(jnp.float32) + norm_back(tok_rows.astype(jnp.float32), d_normed.astype(jnp.float32), gain_f32)
@@ -1022,7 +1028,6 @@
 
             return lax.fori_loop(0, turns, add_turn, jnp.zeros((vocab_dev, d_model), jnp.float32)).astype(jnp.bfloat16)
 
-        g_query = head_columns(g_query)
         grad_table = lax.fori_loop(0, many, many_turns, write_table(pieces, first_plan, my_dev, vocab_dev, jnp.bfloat16))
         g_pe = [g_down[:, kv_rank:kv_rank + HALF_ROPE], g_down[:, kv_rank + ROPE_DIM:kv_rank + ROPE_DIM + HALF_ROPE]]
         grads = (g_down[:, gain_at], g_query, jnp.concatenate([g_down[:, :kv_rank]] + g_pe, axis=COL), g_down[:kv_gain.shape[ROW], kv_gain_at], g_up, g_out)

time: 1010 us -> 1090 us (1.079)
  waiting for transfers between devices: 250 us -> 340 us
  local copies, waits for them, and re-layouts: 49.7 us -> 32.3 us
  Pallas kernels: 496 us -> 507 us
    ppermute x2, waiting for transfers between devices: 6.18 us -> 114 us  [permute_rows(): arrived[source] = [lax.ppermute(direct, 'fsdp', [(source, 0)])]]
    ppermute x7, waiting for transfers between devices: 114 us -> 159 us  [permute_rows(): lax.ppermute(base[hop], 'fsdp', [(dev, dev ^ hop) for dev in range(n_dev)])]
    ppermute x2, waiting for transfers between devices: 39.3 us -> 0.01 us  [permute_rows(): arrived[source].append(lax.ppermute(passed, 'fsdp', [(source - 4, 0)]))]
    reduce_scatter x3 -> x4, waiting for transfers between devices: 43.1 us -> 15.6 us  [side_scatter(): lax.psum_scatter(vals, 'fsdp', scatter_dimension=0, tiled=True, axis_inde...]
    pallas_call x4, Pallas kernels: 69.7 us -> 81.7 us  [grad_rows_of(): pl.pallas_call(kernel, grid=(n_cols // tile,), in_specs=[whole, whole, pa...]
    concatenate x2 -> x0, other arithmetic: 11.1 us -> none  [the longest x1 9.16 us: device_step(): d_w_out_down = jnp.concatenate([d_w_out, d_w_down], axis=COL)]
    unnamed x129 -> x86, local copies, waits for them, and re-layouts: 23.5 us -> 12.6 us
  transfers between devices with their start and end apart: 32 -> 33, of which waited for: 13 -> 12; matrix products, arithmetic and copies ran while one was open for 18% -> 16% of each run, Pallas kernels for 40% -> 47%
where the time goes in v2:
time: 1090 us
  Pallas kernels  507 us (47%)
  waiting for transfers between devices  340 us (31%)
  matrix products  109 us (10%)
  other arithmetic  45 us (4%)
  local copies, waits for them, and re-layouts  32.3 us (3%)
  starting transfers between devices  22 us (2%)
  between operations  16.1 us (1%)
  blocking collectives  11.5 us (1%)
    ppermute x7, waiting for transfers between devices, permute_rows(): lax.ppermute(base[hop], 'fsdp', [(dev, dev ^ hop) for dev in range(n_dev)])  159 us
    pallas_call x1, Pallas kernels, swap_rows(): pl.pallas_call(kernel, out_shape=tuple(out_shape), in_specs=in_specs, out...  151 us
    ppermute x2, waiting for transfers between devices, permute_rows(): arrived[source] = [lax.ppermute(direct, 'fsdp', [(source, 0)])]  114 us
    pallas_call x1, Pallas kernels, write_table(): pl.pallas_call(kernel, out_shape=jax.ShapeDtypeStruct((vocab_dev, width),...  89.4 us
    pallas_call x4, Pallas kernels, grad_rows_of(): pl.pallas_call(kernel, grid=(n_cols // tile,), in_specs=[whole, whole, pa...  81.7 us
    pallas_call x1, Pallas kernels, pick_rows(): pl.pallas_call(kernel, out_shape=jax.ShapeDtypeStruct((n_dev * DEST_ROWS,...  69.9 us
    pallas_call x1, Pallas kernels, attend_pairs(): pl.pallas_call(kernel, grid_spec=pltpu.PrefetchScalarGridSpec(num_scalar_...  67.7 us
    ppermute x5, waiting for transfers between devices, permute_rows(): arrived[source] = [lax.ppermute(heavy, 'fsdp', [(source, 0)])]  43.4 us
  transfers between devices with their start and end apart: 33, of which 12 were waited for; matrix products, arithmetic and copies ran while one was open for 16% of the time, Pallas kernels for 47%

profile of v2, /device:TPU:0, one launch (start us, length us, event | category | flops | bytes accessed | tf_op | source)
XLA Modules:
  0.0 1085.0 jit_solution(10576519964924338223)
XLA Ops:
  16.8 11.5 %all-gather.1 = f32[8,1,3584]{2,1,0:T(1,128)S(1)} all-gather(f32[1,1,3584]{2,1,0:T(1,128)S(1)} %reshape.765), channel_id=2, replica_groups=mesh['dp'=2,'fsdp'=8] {'fsdp'}, dimensions={0}, use_global_device_ids=true | all-gather | bytes 129024 | tf_op jit(solution)/shard_map/all_gather | solution.py:934
  46.0 69.9 %pick_rows.2.refs_0_ = bf16[4992,2048]{1,0:T(8,128)(2,1)} custom-call(s32[4992]{0:T(1024)} %get-tuple-element.1231.tiles_s, s32[1]{0:T(128)} %bitcast.3.dev_s, bf16[12800,2048]{1,0:T(8,128)(2,1)} %table_ref.1, s32[4992,128]{1,0:T(8,128)} %broadcast_in_dim.538.tags_ref), custom_call_target="tpu_custom_call" | custom-call | flops 4000000000 | bytes 100000000 | tf_op jit(solution)/shard_map/pick_rows/pallas_call | solution.py:355
  116.1 151.0 %swap_rows.5 = (bf16[1632,2048]{1,0:T(8,128)(2,1)}, bf16[240,2048]{1,0:T(8,128)(2,1)}, f32[1632,2048]{1,0:T(8,128)}, bf16[1536,2048]{1,0:T(8,128)(2,1)}) custom-call(bf16[4992,2048]{1,0:T(8,128)(2,1)} %pick_rows.2.refs_0_, s32[1,1536]{1,0:T(1,128)S(1)} %and_select_fusion.refs_1_.at_ref, bf16[1536,2048]{1,0:T(8,128)(2,1)} %bitcast.71, ...), custom_call_target="tpu_custom_call" | custom-call | flops 20000000000 | bytes 100000000 | tf_op jit(solution)/shard_map/swap_rows/pallas_call | solution.py:529
  267.5 19.2 %expand_rows.1 = (bf16[1536,2048]{1,0:T(8,128)(2,1)}, bf16[1536,2048]{1,0:T(8,128)(2,1)}, bf16[1536,1024]{1,0:T(8,128)(2,1)}, bf16[1536,1024]{1,0:T(8,128)(2,1)}) custom-call(s32[1]{0:T(128)} %bitcast.2.side_s, s32[1536,128]{1,0:T(8,128)S(1)} %broadcast_in_dim.529.at_ref, bf16[1632,2048]{1,0:T(8,128)(2,1)} %get-tuple-element.1768.rows_ref, ...), custom_call_target="tpu_custom_call" | custom-call | flops 10267656192 | bytes 100000000 | tf_op jit(solution)/shard_map/expand_rows/pallas_call | solution.py:824
  297.5 25.8 %convolution_convert_fusion.1.q_ref = bf16[1536,3072]{1,0:T(8,128)(2,1)} fusion(bf16[1536,2048]{1,0:T(8,128)(2,1)} %get-tuple-element.995, bf16[2048,3072]{1,0:T(8,128)(2,1)} %all-gather.11.cloned.1.call-done), kind=kOutput, calls=%fused_computation.141 | convolution fusion | flops 19332071424 | bytes 28311552 | tf_op jit(solution)/shard_map/dot_general | solution.py:982
  323.3 11.6 %convolution_convert_fusion.kv_ref = bf16[1536,4096]{1,0:T(8,128)(2,1)} fusion(bf16[1536,512]{1,0:T(8,128)(2,1)} %fusion.46, bf16[512,4096]{1,0:T(8,128)(2,1)} %all-gather.13.cloned.1.call-done), kind=kOutput, calls=%fused_computation.134 | convolution fusion | flops 6448742400 | bytes 18350080 | tf_op jit(solution)/shard_map/dot_general | solution.py:981
  334.9 67.7 %attend_pairs.1 = (bf16[1536,2048]{1,0:T(8,128)(2,1)}, bf16[1536,1024]{1,0:T(8,128)(2,1)S(1)}, bf16[1536,1024]{1,0:T(8,128)(2,1)}, bf16[1536,3072]{1,0:T(8,128)(...) custom-call(s32[1]{0:T(128)} %bitcast.2.side_s, bf16[1536,3072]{1,0:T(8,128)(2,1)} %convolution_convert_fusion.1.q_ref, ...), custom_call_target="tpu_custom_call" | custom-call | flops 20000000000 | bytes 100000000 | tf_op jit(solution)/shard_map/attend_pairs/pallas_call | solution.py:221
  411.9 10.8 convolution_convert_fusion.3
  429.0 18.0 %grad_rows_of.4 = f32[1024,2048]{1,0:T(8,128)} custom-call(bf16[1536,1024]{1,0:T(8,128)(2,1)S(1)} %copy-done.7, bf16[1536,1024]{1,0:T(8,128)(2,1)} %collective-permute-done.left_sib, bf16[1536,2048]{1,0:T(8,128)(2,1)S(1)} %bitcast.75, bf16[1536,2048]{1,0:T(8,128)(2,1)} %collective-permute-done.1.right_sib), custom_call_target="tpu_custom_call" | custom-call | flops 12884901888 | bytes 100000000 | tf_op jit(solution)/shard_map/grad_rows_of/pallas_call | solution.py:860
  462.7 24.6 %add_convert_fusion.dn_ref = bf16[1536,2048]{1,0:T(8,128)(2,1)} fusion(f32[1536,2048]{1,0:T(8,128)} %fusion.99, bf16[1536,3072]{1,0:T(8,128)(2,1)} %get-tuple-element.1007.right_own, bf16[2048,3072]{1,0:T(8,128)(2,1)S(1)} %bitcast.93), kind=kOutput, calls=%fused_computation.140 | convolution fusion | flops 19333644288 | bytes 40894464 | tf_op jit(solution)/shard_map/dot_general | solution.py:997
  487.2 24.4 %fold_rows.1 = (f32[144,2048]{1,0:T(8,128)}, f32[144,2048]{1,0:T(8,128)}, f32[144,2048]{1,0:T(8,128)}, f32[144,2048]{1,0:T(8,128)}, f32[144,2048]{1,0:T(8,128)},...) custom-call(s32[1,1536]{1,0:T(1,128)} %copy-done.5, ...), custom_call_target="tpu_custom_call" | custom-call | flops 10267656192 | bytes 100000000 | tf_op jit(solution)/shard_map/fold_rows/pallas_call | solution.py:887
  511.7 13.3 %grad_rows_of.5 = f32[256,4096]{1,0:T(8,128)S(1)} custom-call(bf16[1536,256]{1,0:T(8,128)(2,1)S(1)} %get-tuple-element.1021.left_own, bf16[1536,256]{1,0:T(8,128)(2,1)S(1)} %collective-permute-done.2.left_sib, bf16[1536,4096]{1,0:T(8,128)(2,1)} %get-tuple-element.1004.right_own, bf16[1536,4096]{1,0:T(8,128)(2,1)} %collective-permute-done.3.right_sib), custom_call_target="tpu_custom_call" | custom-call | flops 6442450944 | bytes 100000000 | tf_op jit(solution)/shard_map/grad_rows_of/pallas_call | solution.py:860
  542.0 13.2 %grad_rows_of.6 = f32[1024,640]{1,0:T(8,128)} custom-call(bf16[1536,1024]{1,0:T(8,128)(2,1)S(1)} %copy-done.43, bf16[1536,1024]{1,0:T(8,128)(2,1)} %collective-permute-done.5.left_sib, bf16[1536,640]{1,0:T(8,128)(2,1)S(1)} %pad_maximum_fusion.2.right_own, bf16[1536,640]{1,0:T(8,128)(2,1)} %collective-permute-done.6.right_sib), custom_call_target="tpu_custom_call" | custom-call | flops 4026531840 | bytes 100000000 | tf_op jit(solution)/shard_map/grad_rows_of/pallas_call | solution.py:860
  563.8 12.5 %collective-permute-done.8.refs_2_ = f32[144,2048]{1,0:T(8,128)S(1)} collective-permute-done((f32[144,2048]{1,0:T(8,128)}, f32[144,2048]{1,0:T(8,128)S(1)}, u32[]{:S(2)}, u32[]{:S(2)}) %collective-permute-start.8) | collective-permute-done | bytes 1179680 | tf_op jit(solution)/shard_map/ppermute | solution.py:559
  578.3 27.1 %collective-permute-done.10.refs_4_ = f32[144,2048]{1,0:T(8,128)} collective-permute-done((f32[144,2048]{1,0:T(8,128)}, f32[144,2048]{1,0:T(8,128)}, u32[]{:S(2)}, u32[]{:S(2)}) %collective-permute-start.10) | collective-permute-done | bytes 1179680 | tf_op jit(solution)/shard_map/ppermute | solution.py:559
  605.4 38.4 %collective-permute-done.12.refs_6_ = f32[144,2048]{1,0:T(8,128)} collective-permute-done((f32[144,2048]{1,0:T(8,128)}, f32[144,2048]{1,0:T(8,128)}, u32[]{:S(2)}, u32[]{:S(2)}) %collective-permute-start.12) | collective-permute-done | bytes 1179680 | tf_op jit(solution)/shard_map/ppermute | solution.py:559
  648.1 50.9 %collective-permute-done.18.refs_12_ = f32[144,2048]{1,0:T(8,128)S(1)} collective-permute-done((f32[144,2048]{1,0:T(8,128)}, f32[144,2048]{1,0:T(8,128)S(1)}, u32[]{:S(2)}, u32[]{:S(2)}) %collective-permute-start.18) | collective-permute-done | bytes 1179680 | tf_op jit(solution)/shard_map/ppermute | solution.py:559
  702.6 29.0 %collective-permute-done.22.refs_15_ = f32[144,2048]{1,0:T(8,128)} collective-permute-done((f32[144,2048]{1,0:T(8,128)}, f32[144,2048]{1,0:T(8,128)}, u32[]{:S(2)}, u32[]{:S(2)}) %collective-permute-start.22) | collective-permute-done | bytes 1179680 | tf_op jit(solution)/shard_map/ppermute | solution.py:559
  736.6 111.1 %collective-permute-done.23.refs_16_ = f32[240,2048]{1,0:T(8,128)} collective-permute-done((f32[240,2048]{1,0:T(8,128)S(1)}, f32[240,2048]{1,0:T(8,128)}, u32[]{:S(2)}, u32[]{:S(2)}) %collective-permute-start.23) | collective-permute-done | bytes 1966112 | tf_op jit(solution)/shard_map/ppermute | solution.py:554
  857.2 37.2 %grad_rows_of.7 = f32[1024,3072]{1,0:T(8,128)} custom-call(bf16[1536,1024]{1,0:T(8,128)(2,1)S(1)} %copy-done.44, bf16[1536,1024]{1,0:T(8,128)(2,1)} %collective-permute-done.5.left_sib, bf16[1536,3072]{1,0:T(8,128)(2,1)} %get-tuple-element.1007.right_own, bf16[1536,3072]{1,0:T(8,128)(2,1)} %collective-permute-done.7.right_sib, bf16[384,384]{1,0:T(8,128)(2,1)S(1)} %copy-done.3), custom_call_target="tpu_custom_call" | custom-call | flops 19327352832 | bytes 100000000 | tf_op jit(solution)/shard_map/grad_rows_of/pallas_call | solution.py:860
  894.4 20.3 %fusion.40 = bf16[1536,2048]{1,0:T(8,128)(2,1)} fusion(bf16[1536,2048]{1,0:T(8,128)(2,1)} %get-tuple-element.1022, bf16[1536,2048]{1,0:T(8,128)(2,1)} %get-tuple-element.1028, bf16[2048,2048]{1,0:T(8,128)(2,1)} %all-gather.7.cloned.1.call-done.refs_3_), kind=kOutput, calls=%fused_computation.139 | convolution fusion | flops 12894339072 | bytes 27262976 | tf_op jit(solution)/shard_map/dot_general | solution.py:1018
  914.7 41.9 %collective-permute-done.17.refs_11_ = f32[480,2048]{1,0:T(8,128)} collective-permute-done((f32[480,2048]{1,0:T(8,128)}, f32[480,2048]{1,0:T(8,128)}, u32[]{:S(2)}, u32[]{:S(2)}) %collective-permute-start.17) | collective-permute-done | bytes 3932192 | tf_op jit(solution)/shard_map/ppermute | solution.py:556
  964.9 89.4 %write_table.5 = bf16[12800,2048]{1,0:T(8,128)(2,1)} custom-call(s32[800]{0:T(1024)} %reshape.762.firsts_s, s32[800]{0:T(1024)} %reshape.763.counts_s, s32[1]{0:T(128)} %bitcast.3.dev_s, f32[144,2048]{1,0:T(8,128)} %get-tuple-element.1011.refs_0_, f32[480,2048]{1,0:T(8,128)} %constant_dynamic-update-slice_fusion.refs_1_, f32[144,2048]{1,0:T(8,128)} %copy-done.19, ...), custom_call_target="tpu_custom_call" | custom-call | flops 4000000000 | bytes 100000000 | tf_op jit(solution)/shard_map/write_table/pallas_call | solution.py:762
  1062.2 15.6 %reduce-scatter.7.cloned.1.call-done = f32[256,3072]{1,0:T(8,128)} async-done(((f32[1024,3072]{1,0:T(8,128)}), f32[256,3072]{1,0:T(8,128)}) %reduce-scatter.7.cloned.1.call-update) | async-done | bytes 3145744 | tf_op jit(solution)/shard_map/reduce_scatter | solution.py:904
  (240 shorter events, 134.6 us)
Async XLA Ops:
  7.2 109.0 %all-gather.7.cloned.1.call-start = ((), (), s32[]{:S(2)}) async-start(), calls=%async_computation.4 | async-start | bytes 9437184 | tf_op jit(solution)/shard_map/all_gather | solution.py:944
  7.9 279.1 %all-gather.9.cloned.1.call-start = ((), (), s32[]{:S(2)}) async-start(), calls=%async_computation.5 | async-start | bytes 2949120 | tf_op jit(solution)/shard_map/all_gather | solution.py:947
  35.7 261.8 %all-gather.11.cloned.1.call-start = ((), (), s32[]{:S(2)}) async-start(), calls=%async_computation.6 | async-start | bytes 14155776 | tf_op jit(solution)/shard_map/all_gather | solution.py:946
  36.5 286.8 %all-gather.13.cloned.1.call-start = ((), (), s32[]{:S(2)}) async-start(), calls=%async_computation.7 | async-start | bytes 4718592 | tf_op jit(solution)/shard_map/all_gather | solution.py:978
  36.5 386.2 %collective-permute-start.1 = (bf16[1536,2048]{1,0:T(8,128)(2,1)}, bf16[1536,2048]{1,0:T(8,128)(2,1)}, u32[]{:S(2)}, u32[]{:S(2)}) collective-permute-start(bf16[1536,2048]{1,0:T(8,128)(2,1)} %bitcast.70), channel_id=1, source_target_pairs={{0,1},{1,0},{2,3},{3,2},{4,5},{5,4},{6,7},{7,6},{8,9},{9,8},{10,11... | collective-permute-start | bytes 18874376 | tf_op jit(solution)/shard_map/ppermute | solution.py:899
  267.2 788.5 %reduce-scatter.5.cloned.1.call-start = ((), (), s32[]{:S(2)}) async-start(), calls=%async_computation.8 | async-start | bytes 3276800 | tf_op jit(solution)/shard_map/reduce_scatter | solution.py:904
  405.0 106.6 %collective-permute-start.3 = (bf16[1536,4096]{1,0:T(8,128)(2,1)}, bf16[1536,4096]{1,0:T(8,128)(2,1)}, u32[]{:S(2)}, u32[]{:S(2)}) collective-permute-start(bf16[1536,4096]{1,0:T(8,128)(2,1)} %get-tuple-element.1004.right_own), channel_id=1, source_target_pairs={{0,1},{1,0},{2,3},{3,2},{4,5},{5,4},{6,7},{7,6},{8,9},{9,8},{10,11... | collective-permute-start | bytes 37748744 | tf_op jit(solution)/shard_map/ppermute | solution.py:899
  411.4 100.3 %collective-permute-start.2 = (bf16[1536,256]{1,0:T(8,128)(2,1)}, bf16[1536,256]{1,0:T(8,128)(2,1)S(1)}, u32[]{:S(2)}, u32[]{:S(2)}) collective-permute-start(bf16[1536,256]{1,0:T(8,128)(2,1)} %get-tuple-element.1215), channel_id=1, source_target_pairs={{0,1},{1,0},{2,3},{3,2},{4,5},{5,4},{6,7},{7,6},{8,9},{9,8},{10,11... | collective-permute-start | bytes 2359304 | tf_op jit(solution)/shard_map/ppermute | solution.py:899
  411.4 130.5 %collective-permute-start.5 = (bf16[1536,1024]{1,0:T(8,128)(2,1)}, bf16[1536,1024]{1,0:T(8,128)(2,1)}, u32[]{:S(2)}, u32[]{:S(2)}) collective-permute-start(bf16[1536,1024]{1,0:T(8,128)(2,1)} %get-tuple-element.1025), channel_id=1, source_target_pairs={{0,1},{1,0},{2,3},{3,2},{4,5},{5,4},{6,7},{7,6},{8,9},{9,8},{10,11... | collective-permute-start | bytes 9437192 | tf_op jit(solution)/shard_map/ppermute | solution.py:899
  454.4 87.6 %collective-permute-start.6 = (bf16[1536,640]{1,0:T(8,128)(2,1)S(1)}, bf16[1536,640]{1,0:T(8,128)(2,1)}, u32[]{:S(2)}, u32[]{:S(2)}) collective-permute-start(bf16[1536,640]{1,0:T(8,128)(2,1)S(1)} %pad_maximum_fusion.2.right_own), channel_id=1, source_target_pairs={{0,1},{1,0},{2,3},{3,2},{4,5},{5,4},{6,7},{7,6},{8,9},{9,8},{10,11... | collective-permute-start | bytes 5898248 | tf_op jit(solution)/shard_map/ppermute | solution.py:899
  559.1 503.1 %reduce-scatter.11.cloned.1.call-start = ((), (), s32[]{:S(2)}) async-start(), calls=%async_computation.11 | async-start | bytes 10485760 | tf_op jit(solution)/shard_map/reduce_scatter | solution.py:904
  559.7 502.6 %reduce-scatter.9.cloned.1.call-start = ((), (), s32[]{:S(2)}) async-start(), calls=%async_computation.10 | async-start | bytes 5242880 | tf_op jit(solution)/shard_map/reduce_scatter | solution.py:904
  559.7 296.1 %collective-permute-start.7 = (bf16[1536,3072]{1,0:T(8,128)(2,1)}, bf16[1536,3072]{1,0:T(8,128)(2,1)}, u32[]{:S(2)}, u32[]{:S(2)}) collective-permute-start(bf16[1536,3072]{1,0:T(8,128)(2,1)} %get-tuple-element.1007.right_own), channel_id=1, source_target_pairs={{0,1},{1,0},{2,3},{3,2},{4,5},{5,4},{6,7},{7,6},{8,9},{9,8},{10,11... | collective-permute-start | bytes 28311560 | tf_op jit(solution)/shard_map/ppermute | solution.py:899
  576.3 125.0 %collective-permute-start.20 = (f32[240,2048]{1,0:T(8,128)}, f32[240,2048]{1,0:T(8,128)}, u32[]{:S(2)}, u32[]{:S(2)}) collective-permute-start(f32[240,2048]{1,0:T(8,128)} %get-tuple-element.1020), channel_id=1, source_target_pairs={{6,2},{7,3},{14,10},{15,11}} | collective-permute-start | bytes 5898248 | tf_op jit(solution)/shard_map/ppermute | solution.py:551
  578.3 499.5 %reduce-scatter.7.cloned.1.call-start = ((), (), s32[]{:S(2)}) async-start(), calls=%async_computation.9 | async-start | bytes 15728640 | tf_op jit(solution)/shard_map/reduce_scatter | solution.py:904
  646.8 200.9 %collective-permute-start.23 = (f32[240,2048]{1,0:T(8,128)S(1)}, f32[240,2048]{1,0:T(8,128)}, u32[]{:S(2)}, u32[]{:S(2)}) collective-permute-start(f32[240,2048]{1,0:T(8,128)S(1)} %copy-done.17), channel_id=1, source_target_pairs={{7,0},{15,8}} | collective-permute-start | bytes 5898248 | tf_op jit(solution)/shard_map/ppermute | solution.py:554
  700.0 151.9 %collective-permute-start.19 = (f32[240,2048]{1,0:T(8,128)S(1)}, f32[240,2048]{1,0:T(8,128)}, u32[]{:S(2)}, u32[]{:S(2)}) collective-permute-start(f32[240,2048]{1,0:T(8,128)S(1)} %copy-done.17), channel_id=1, source_target_pairs={{6,0},{14,8}} | collective-permute-start | bytes 5898248 | tf_op jit(solution)/shard_map/ppermute | solution.py:554
  701.3 151.9 %collective-permute-start.24 = (f32[240,2048]{1,0:T(8,128)}, f32[240,2048]{1,0:T(8,128)}, u32[]{:S(2)}, u32[]{:S(2)}) collective-permute-start(f32[240,2048]{1,0:T(8,128)} %collective-permute-done.20), channel_id=1, source_target_pairs={{3,0},{11,8}} | collective-permute-start | bytes 5898248 | tf_op jit(solution)/shard_map/ppermute | solution.py:558
  731.6 122.9 %collective-permute-start.21 = (f32[240,2048]{1,0:T(8,128)}, f32[240,2048]{1,0:T(8,128)}, u32[]{:S(2)}, u32[]{:S(2)}) collective-permute-start(f32[240,2048]{1,0:T(8,128)} %collective-permute-done.20), channel_id=1, source_target_pairs={{2,0},{10,8}} | collective-permute-start | bytes 5898248 | tf_op jit(solution)/shard_map/ppermute | solution.py:558
  847.7 108.8 %collective-permute-start.17 = (f32[480,2048]{1,0:T(8,128)}, f32[480,2048]{1,0:T(8,128)}, u32[]{:S(2)}, u32[]{:S(2)}) collective-permute-start(f32[480,2048]{1,0:T(8,128)} %constant_dynamic-update-slice_fusion.refs_1_), channel_id=1, source_target_pairs={{5,0},{13,8}} | collective-permute-start | bytes 11796488 | tf_op jit(solution)/shard_map/ppermute | solution.py:556
  851.9 106.2 %collective-permute-start.15 = (f32[480,2048]{1,0:T(8,128)}, f32[480,2048]{1,0:T(8,128)}, u32[]{:S(2)}, u32[]{:S(2)}) collective-permute-start(f32[480,2048]{1,0:T(8,128)} %constant_dynamic-update-slice_fusion.refs_1_), channel_id=1, source_target_pairs={{4,0},{12,8}} | collective-permute-start | bytes 11796488 | tf_op jit(solution)/shard_map/ppermute | solution.py:556
  853.2 104.9 %collective-permute-start.13 = (f32[480,2048]{1,0:T(8,128)}, f32[480,2048]{1,0:T(8,128)}, u32[]{:S(2)}, u32[]{:S(2)}) collective-permute-start(f32[480,2048]{1,0:T(8,128)} %constant_dynamic-update-slice_fusion.refs_1_), channel_id=1, source_target_pairs={{3,0},{11,8}} | collective-permute-start | bytes 11796488 | tf_op jit(solution)/shard_map/ppermute | solution.py:556
  854.5 103.6 %collective-permute-start.11 = (f32[480,2048]{1,0:T(8,128)}, f32[480,2048]{1,0:T(8,128)}, u32[]{:S(2)}, u32[]{:S(2)}) collective-permute-start(f32[480,2048]{1,0:T(8,128)} %constant_dynamic-update-slice_fusion.refs_1_), channel_id=1, source_target_pairs={{2,0},{10,8}} | collective-permute-start | bytes 11796488 | tf_op jit(solution)/shard_map/ppermute | solution.py:556
  855.8 102.3 %collective-permute-start.9 = (f32[480,2048]{1,0:T(8,128)}, f32[480,2048]{1,0:T(8,128)}, u32[]{:S(2)}, u32[]{:S(2)}) collective-permute-start(f32[480,2048]{1,0:T(8,128)} %constant_dynamic-update-slice_fusion.refs_1_), channel_id=1, source_target_pairs={{1,0},{9,8}} | collective-permute-start | bytes 11796488 | tf_op jit(solution)/shard_map/ppermute | solution.py:556
  (46 other events, 1949.9 us)
Sparse Core Ops, SparseCore 0:
  9.8 53.7 all-gather.6
  66.0 26.2 all-gather.8
  94.7 118.0 all-gather.10
  267.3 33.4 all-gather.12
  559.2 57.6 reduce-scatter.4
  620.3 197.1 reduce-scatter.10
  821.1 79.5 reduce-scatter.8
  961.8 115.9 reduce-scatter.6
